TPU v7x, 32 devices: a whole 2x2x4 slice. The times are simulated.
32 devices in a mesh: src: 4 (over y, x), rcv: 8 (over z, core).
Axes of the slice: x: 2, y: 2, z: 4, core: 2. Of those that a mesh axis runs over, the one named last changes fastest.
Arguments:
- wavefield: float32 [2, 16, 2048, 2048], P(None, None, 'rcv', 'src')
- surface_band: float32 [2, 2048, 1024], P(None, 'rcv'), may hold values from -0.75 to 0.75
- band_shift: int32 [32], P('rcv'), may hold values from -16 to 16
- trace_mask: int32 [2048], P('rcv'), may hold values 0 or 1
- shot_taper: float32 [5], replicated, may hold values from 0.2 to 1
Outputs:
- multiples: float32 [2, 16, 2048, 2048], P(None, None, 'rcv', 'src')
- primaries: float32 [2, 16, 2048, 2048], P(None, None, 'rcv', 'src')
All inputs are finite; a program needn't handle non-finite values. No bound on the sum of `trace_mask` on one device may be relied on, other than what follows from the above.
Results may differ from a plain program's by a relative error of at most 0.0003.
Values sent between devices are 32-bit elements; how exact they have to be, the bound alone decides.
A program may use at most 192 MiB of HBM per device.

v0:
```python
import functools

import jax
import jax.numpy as jnp
from jax import lax
from jax.experimental import pallas as pl
from jax.experimental.pallas import tpu as pltpu
from jax.sharding import PartitionSpec as P

APER = 64
SHIFT = 16
BLOCK = 64
SHALF = 2
LANES = 128
HALO = APER // 2 + SHIFT
CHUNKS = 2
MESH = pl.DeviceIdType.MESH


def shifted(cells, axis, step):
    count = lax.axis_size(axis)
    ends = count - 1
    if step > 0:
        pairs = [(i, i + 1) for i in range(ends)]
    else:
        pairs = [(i + 1, i) for i in range(ends)]
    return lax.ppermute(cells, axis, pairs)


def split(cells):
    high = cells.astype(jnp.bfloat16)
    low = (cells - high.astype(jnp.float32)).astype(jnp.bfloat16)
    return high, low


def predict_kernel(first, shift_ref, taper_ref, wave_ref, mask_ref, above_ref, below_ref, side_ref, band_ref, *refs):
    mult_ref, energy_ref, rows_ref = refs[-3:]
    step = pl.program_id(0)
    here = first + step
    receivers, shots = wave_ref.shape[2:]
    width = shots + LANES

    data = jnp.float32(0)
    for x in range(2):
        wave = wave_ref[x, 0]
        data = data + jnp.sum(wave * wave)
        rows_ref[x, HALO : HALO + receivers, :shots] = wave * mask_ref[...]
        rows_ref[x, :HALO, :shots] = above_ref[x, 0]
        rows_ref[x, HALO + receivers : receivers + 2 * HALO, :shots] = below_ref[x, 0]
        rows_ref[x, : receivers + 2 * HALO, shots:] = side_ref[x, 0]

    odd = here % 2 == 1
    lane = lax.broadcasted_iota(jnp.int32, (BLOCK, LANES), 1)

    def skewed(x, index):
        taps = band_ref[x, index * BLOCK : (index + 1) * BLOCK, :]
        taps = jnp.where(odd, pltpu.roll(taps, LANES - APER, 1), taps)
        taps = jnp.where(lane < APER, taps, 0.0)
        return pltpu.roll(taps, 0, 1, stride=1, stride_axis=0)

    def near(x, whole, rest):
        tall = rows_ref[x, pl.ds(whole, 2 * BLOCK + 8), :]
        return pltpu.roll(tall, (2 * BLOCK + 8 - rest) % (2 * BLOCK + 8), 0)[: 2 * BLOCK]

    total = jnp.zeros((8, shots), jnp.float32)
    for index in range(receivers // BLOCK):
        start = index * BLOCK + HALO - APER // 2 + shift_ref[index]
        rest = start & 7
        whole = pl.multiple_of(start - rest, 8)
        window = jnp.concatenate([near(x, whole, rest) for x in range(2)], axis=0)
        high, low = split(window)
        real, imag = skewed(0, index), skewed(1, index)
        weights = jnp.concatenate(
            [jnp.concatenate([real, -imag], axis=1), jnp.concatenate([imag, real], axis=1)], axis=0
        )
        weights_high, weights_low = split(weights)
        both = jnp.concatenate([weights_high, weights_low], axis=0)
        upper = jnp.dot(both, high, preferred_element_type=jnp.float32)
        lower = jnp.dot(weights_high, low, preferred_element_type=jnp.float32)
        pred = upper[: 2 * BLOCK] + (upper[2 * BLOCK :] + lower)
        mult = taper_ref[SHALF] * pred[:, :shots]
        for u in range(2 * SHALF + 1):
            if u != SHALF:
                mult = mult + taper_ref[u] * pltpu.roll(pred, (SHALF - u) % width, 1)[:, :shots]
        mult_ref[0, 0, index * BLOCK : (index + 1) * BLOCK, :] = mult[:BLOCK]
        mult_ref[1, 0, index * BLOCK : (index + 1) * BLOCK, :] = mult[BLOCK:]
        total = total + jnp.sum((mult * mult).reshape(-1, 8, shots), axis=0)

    row = lax.broadcasted_iota(jnp.int32, (8, LANES), 0)
    col = lax.broadcasted_iota(jnp.int32, (8, LANES), 1)
    news = jnp.where(row == 0, data, jnp.sum(total))
    news = jnp.where((row < 2) & (col == here), news, 0.0)

    @pl.when(step == 0)
    def _():
        energy_ref[...] = jnp.zeros_like(energy_ref)

    energy_ref[...] += news


def predict(first, count, wave, mask, above, below, side, band, band_shift, shot_taper, mult):
    _, slices, receivers, shots = wave.shape
    in_specs = [
        pl.BlockSpec(memory_space=pltpu.SMEM),
        pl.BlockSpec(memory_space=pltpu.SMEM),
        pl.BlockSpec((2, 1, receivers, shots), lambda g: (0, first + g, 0, 0)),
        pl.BlockSpec((receivers, 1), lambda g: (0, 0)),
        pl.BlockSpec((2, 1, HALO, shots), lambda g: (0, g, 0, 0)),
        pl.BlockSpec((2, 1, HALO, shots), lambda g: (0, g, 0, 0)),
        pl.BlockSpec((2, 1, receivers + 2 * HALO, LANES), lambda g: (0, first + g, 0, 0)),
        pl.BlockSpec((2, receivers, LANES), lambda g: (0, 0, (first + g) // 2)),
    ]
    args = [band_shift, shot_taper, wave, mask, above, below, side, band]
    aliases = {}
    if mult is not None:
        in_specs.append(pl.BlockSpec(memory_space=pl.ANY))
        aliases = {len(args): 0}
        args.append(mult)
    flops = 3 * 2 * 4 * BLOCK * 4 * BLOCK * count * (receivers // BLOCK) * (shots + LANES)
    return pl.pallas_call(
        functools.partial(predict_kernel, first),
        grid=(count,),
        in_specs=in_specs,
        out_specs=[
            pl.BlockSpec((2, 1, receivers, shots), lambda g: (0, first + g, 0, 0)),
            pl.BlockSpec((8, LANES), lambda g: (0, 0)),
        ],
        out_shape=[
            jax.ShapeDtypeStruct(wave.shape, jnp.float32),
            jax.ShapeDtypeStruct((8, LANES), jnp.float32),
        ],
        scratch_shapes=[pltpu.VMEM((2, receivers + 2 * HALO + 8, shots + LANES), jnp.float32)],
        input_output_aliases=aliases,
        cost_estimate=pl.CostEstimate(
            flops=flops, bytes_accessed=count * receivers * shots * 20, transcendentals=0
        ),
        compiler_params=pltpu.CompilerParams(
            dimension_semantics=("arbitrary",), vmem_limit_bytes=48 * 2**20
        ),
        name=f"predict{first}",
    )(*args)


def gain_kernel(axes, *refs):
    energies, (gain_ref, mine, plane, space, local_sem, send_a, recv_a, send_b, recv_b) = refs[:-9], refs[-9:]
    (slow, slow_count), (fast, fast_count) = axes
    slow_me, fast_me = lax.axis_index(slow), lax.axis_index(fast)

    def slow_peer(d):
        return {slow: lax.rem(slow_me + d, slow_count)}

    def fast_peer(d):
        return {fast: lax.rem(fast_me + d, fast_count)}

    barrier = pltpu.get_barrier_semaphore()
    for d in range(1, slow_count):
        pl.semaphore_signal(barrier, inc=1, device_id=slow_peer(d), device_id_type=MESH)
    for d in range(1, fast_count):
        pl.semaphore_signal(barrier, inc=1, device_id=fast_peer(d), device_id_type=MESH)
    total = energies[0][...]
    for other in energies[1:]:
        total = total + other[...]
    mine[...] = total
    own = pltpu.make_async_copy(mine, plane.at[0], local_sem)
    own.start()
    pl.semaphore_wait(barrier, slow_count + fast_count - 2)

    copies = []
    for d in range(1, slow_count):
        copy = pltpu.make_async_remote_copy(
            src_ref=mine, dst_ref=plane.at[d], send_sem=send_a.at[d], recv_sem=recv_a.at[d],
            device_id=slow_peer(d), device_id_type=MESH,
        )
        copy.start()
        copies.append(copy)
    own.wait()
    for copy in copies:
        copy.wait()
    copies = []
    for d in range(1, fast_count):
        copy = pltpu.make_async_remote_copy(
            src_ref=plane, dst_ref=space.at[d - 1], send_sem=send_b.at[d], recv_sem=recv_b.at[d],
            device_id=fast_peer(d), device_id_type=MESH,
        )
        copy.start()
        copies.append(copy)
    total = jnp.sum(plane[...], axis=0)
    for copy in copies:
        copy.wait()
    for d in range(fast_count - 1):
        total = total + jnp.sum(space[d], axis=0)
    data = jnp.broadcast_to(total[0:1], total.shape)
    pred = jnp.broadcast_to(total[1:2], total.shape)
    gain_ref[...] = jnp.sqrt((data + 1e-06) / (pred + 1e-06))


def gains(energies, axes, identity):
    slow_count, fast_count = axes[0][1], axes[1][1]
    return pl.pallas_call(
        functools.partial(gain_kernel, axes),
        in_specs=[pl.BlockSpec(memory_space=pltpu.VMEM)] * len(energies),
        out_specs=pl.BlockSpec(memory_space=pltpu.VMEM),
        out_shape=jax.ShapeDtypeStruct((8, LANES), jnp.float32),
        scratch_shapes=[
            pltpu.VMEM((8, LANES), jnp.float32),
            pltpu.VMEM((slow_count, 8, LANES), jnp.float32),
            pltpu.VMEM((fast_count - 1, slow_count, 8, LANES), jnp.float32),
            pltpu.SemaphoreType.DMA,
            pltpu.SemaphoreType.DMA((slow_count,)),
            pltpu.SemaphoreType.DMA((slow_count,)),
            pltpu.SemaphoreType.DMA((fast_count,)),
            pltpu.SemaphoreType.DMA((fast_count,)),
        ],
        cost_estimate=pl.CostEstimate(flops=1000, bytes_accessed=8 * 2**20, transcendentals=0),
        compiler_params=pltpu.CompilerParams(collective_id=identity, has_side_effects=True),
        name=f"gains{identity}",
    )(*energies)


def subtract_kernel(first, gain_ref, wave_ref, mult_ref, *refs):
    prim_ref = refs[-1]
    here = first + pl.program_id(0)
    col = lax.broadcasted_iota(jnp.int32, (1, LANES), 1)
    gain = jnp.sum(jnp.where(col == here, gain_ref[0:1, :], 0.0))
    prim_ref[...] = wave_ref[...] - gain * mult_ref[...]


def subtract(first, count, gain, wave, mult, prim):
    _, slices, receivers, shots = wave.shape
    block = pl.BlockSpec((2, 1, receivers, shots), lambda g: (0, first + g, 0, 0))
    in_specs = [pl.BlockSpec((8, LANES), lambda g: (0, 0)), block, block]
    args = [gain, wave, mult]
    aliases = {}
    if prim is not None:
        in_specs.append(pl.BlockSpec(memory_space=pl.ANY))
        aliases = {len(args): 0}
        args.append(prim)
    return pl.pallas_call(
        functools.partial(subtract_kernel, first),
        grid=(count,),
        in_specs=in_specs,
        out_specs=block,
        out_shape=jax.ShapeDtypeStruct(wave.shape, jnp.float32),
        input_output_aliases=aliases,
        cost_estimate=pl.CostEstimate(
            flops=0, bytes_accessed=count * receivers * shots * 24, transcendentals=0
        ),
        compiler_params=pltpu.CompilerParams(
            dimension_semantics=("arbitrary",), vmem_limit_bytes=48 * 2**20
        ),
        name=f"subtract{first}",
    )(*args)


def per_device(wavefield, surface_band, band_shift, trace_mask, shot_taper):
    _, slices, receivers, shots = wavefield.shape
    mask = trace_mask.astype(jnp.float32)
    size = slices // CHUNKS

    halos = []
    for c in range(CHUNKS):
        part = wavefield[:, c * size : (c + 1) * size]
        tail = part[:, :, receivers - HALO :] * mask[None, None, receivers - HALO :, None]
        head = part[:, :, :HALO] * mask[None, None, :HALO, None]
        halos.append((shifted(tail, "rcv", 1), shifted(head, "rcv", -1)))

    pick = jnp.eye(SHALF, LANES, dtype=jnp.float32)
    turn = functools.partial(jnp.einsum, precision=lax.Precision.HIGHEST)
    first = turn("cl,xfrl->xfcr", pick, wavefield[..., :LANES]) * mask
    last = turn("cl,xfrl->xfcr", jnp.roll(pick, -SHALF, 1), wavefield[..., shots - LANES :]) * mask
    after = shifted(first, "src", -1)
    before = shifted(last, "src", 1)
    sides = jnp.concatenate([after, before], axis=2)
    sides = jnp.concatenate(
        [
            shifted(sides[..., receivers - HALO :], "rcv", 1),
            sides,
            shifted(sides[..., :HALO], "rcv", -1),
        ],
        axis=3,
    )
    place = jnp.concatenate([pick, jnp.roll(pick, -SHALF, 1)], axis=0)
    side = turn("xfcr,cl->xfrl", sides, place)
    column = mask[:, None]
    mult = None
    energies = []
    for c in range(CHUNKS):
        mult, energy = predict(
            c * size, size, wavefield, column, *halos[c], side, surface_band, band_shift, shot_taper, mult
        )
        energies.append(energy)
    axes = (("src", lax.axis_size("src")), ("rcv", lax.axis_size("rcv")))
    gain = gains(energies, axes, 1)
    prim = subtract(0, slices, gain, wavefield, mult, None)
    return (mult, prim)


def solution(mesh):
    in_specs = (P(None, None, "rcv", "src"), P(None, "rcv", None), P("rcv"), P("rcv"), P())
    out_specs = (P(None, None, "rcv", "src"), P(None, None, "rcv", "src"))
    return jax.shard_map(
        per_device, mesh=mesh, in_specs=in_specs, out_specs=out_specs, check_vma=False
    )
```

profile of v0, /device:TPU:0, one launch (start us, length us, event | category | flops | bytes accessed | tf_op | source)
XLA Modules:
  0.0 167.8 jit_solution(1379211558326909645)
XLA Ops:
  0.6 0.7 convert_element_type.10
  1.3 0.1 fusion.35
  1.4 6.3 %slice_multiply_fusion = (f32[2,8,48,512]{3,2,1,0:T(8,128)}, f32[2,8,48,512]{3,2,1,0:T(8,128)}, f32[2,8,48,512]{3,2,1,0:T(8,128)}, f32[2,8,48,512]{3,2,1,0:T(8,128)}) fusion(f32[2,16,256,512]{3,2,1,0:T(8,128)} %wave_ref.5, f32[48]{0:T(128)S(1)} %get-tuple-element.18, f32[48]{0:T(128)S(1)} %get-tuple-element.19), kind=kLoop, calls=%fused_computation.4 | loop fusion | flops 1572864 | bytes 12583296 | tf_op jit(solution)/shard_map/mul | solution.py:264
  7.7 1.3 collective-permute-start.7
  8.9 4.2 %collective-permute-start.6 = (f32[2,8,48,512]{3,2,1,0:T(8,128)}, f32[2,8,48,512]{3,2,1,0:T(8,128)}, u32[]{:S(2)}, u32[]{:S(2)}) collective-permute-start(f32[2,8,48,512]{3,2,1,0:T(8,128)} %get-tuple-element.15), channel_id=1, source_target_pairs={{0,1},{1,2},{2,3},{3,4},{4,5},{5,6},{6,7},{8,9},{9,10},{10,11},{11... | collective-permute-start | bytes 4718600 | tf_op jit(solution)/shard_map/ppermute | solution.py:27
  13.2 4.2 %fusion.7 = f32[2,16,2,256]{3,2,1,0:T(2,128)S(1)} fusion(f32[2,16,256,512]{3,2,1,0:T(8,128)} %wave_ref.5, f32[256]{0:T(256)S(1)} %convert_element_type.10), kind=kOutput, calls=%fused_computation.9 | convolution fusion | flops 25182464 | bytes 4260864 | tf_op jit(solution)/shard_map/cl,xfrl->xfcr/dot_general | solution.py:269
  17.4 1.3 collective-permute-start.2
  18.7 1.3 collective-permute-start.1
  20.0 4.1 %collective-permute-start = (f32[2,8,48,512]{3,2,1,0:T(8,128)}, f32[2,8,48,512]{3,2,1,0:T(8,128)S(1)}, u32[]{:S(2)}, u32[]{:S(2)}) collective-permute-start(f32[2,8,48,512]{3,2,1,0:T(8,128)} %get-tuple-element.14), channel_id=1, source_target_pairs={{0,1},{1,2},{2,3},{3,4},{4,5},{5,6},{6,7},{8,9},{9,10},{10,11},{11... | collective-permute-start | bytes 4718600 | tf_op jit(solution)/shard_map/ppermute | solution.py:27
  24.1 0.1 slice.53
  24.2 5.7 %fusion.13 = f32[2,16,2,256]{3,2,1,0:T(2,128)S(1)} fusion(f32[2,16,256,512]{3,2,1,0:T(8,128)} %wave_ref.5, f32[256]{0:T(256)S(1)} %convert_element_type.10, f32[2,2]{1,0:T(2,128)S(1)} %bitcast.22, f32[2,126]{1,0:T(2,128)S(1)} %slice.53), kind=kOutput, calls=%fused_computation.11 | convolution fusion | flops 25182464 | bytes 4261888 | tf_op jit(solution)/shard_map/cl,xfrl->xfcr/dot_general | solution.py:270
  29.8 0.0 collective-permute-done.2
  29.8 4.5 %collective-permute-start.3 = (f32[2,16,2,256]{3,2,1,0:T(2,128)S(1)}, f32[2,16,2,256]{3,2,1,0:T(2,128)S(1)}, u32[]{:S(2)}, u32[]{:S(2)}) collective-permute-start(f32[2,16,2,256]{3,2,1,0:T(2,128)S(1)} %fusion.13), channel_id=1, source_target_pairs={{0,8},{8,16},{16,24},{1,9},{9,17},{17,25},{2,10},{10,18},{18,26},{... | collective-permute-start | bytes 196616 | tf_op jit(solution)/shard_map/ppermute | solution.py:27
  34.4 2.1 %collective-permute-done.3 = f32[2,16,2,256]{3,2,1,0:T(2,128)S(1)} collective-permute-done((f32[2,16,2,256]{3,2,1,0:T(2,128)S(1)}, f32[2,16,2,256]{3,2,1,0:T(2,128)S(1)}, u32[]{:S(2)}, u32[]{:S(2)}) %collective-permute-start.3) | collective-permute-done | bytes 65568 | tf_op jit(solution)/shard_map/ppermute | solution.py:27
  36.4 0.7 fusion.24
  37.2 2.4 %collective-permute-start.4 = (f32[2,16,4,48]{3,2,1,0:T(4,128)S(1)}, f32[2,16,4,48]{3,2,1,0:T(4,128)S(1)}, u32[]{:S(2)}, u32[]{:S(2)}) collective-permute-start(f32[2,16,4,48]{3,2,1,0:T(4,128)S(1)} %get-tuple-element.16), channel_id=1, source_target_pairs={{0,1},{1,2},{2,3},{3,4},{4,5},{5,6},{6,7},{8,9},{9,10},{10,11},{11... | collective-permute-start | bytes 73736 | tf_op jit(solution)/shard_map/ppermute | solution.py:27
  39.6 0.9 collective-permute-done.4
  40.5 1.5 collective-permute-start.5
  41.9 0.1 copy.9.mask_ref
  42.1 0.0 copy-start
  42.1 0.0 copy-start.4
  42.1 0.0 copy-start.5
  42.1 10.5 %collective-permute-done.5 = f32[2,16,4,48]{3,2,1,0:T(4,128)S(1)} collective-permute-done((f32[2,16,4,48]{3,2,1,0:T(4,128)}, f32[2,16,4,48]{3,2,1,0:T(4,128)S(1)}, u32[]{:S(2)}, u32[]{:S(2)}) %collective-permute-start.5) | collective-permute-done | bytes 24608 | tf_op jit(solution)/shard_map/ppermute | solution.py:27
  52.6 11.4 %fusion.16.side_ref = f32[2,16,352,128]{3,2,1,0:T(8,128)} fusion(f32[2,16,4,48]{3,2,1,0:T(4,128)S(1)} %collective-permute-done.5, f32[2,16,2,256]{3,2,1,0:T(2,128)S(1)} %collective-permute-done.3, f32[2,16,2,256]{3,2,1,0:T(2,128)S(1)} %collective-permute-done.2, f32[2,16,4,48]{3,2,1,0:T(4,128)S(1)} %collective-permute-done.4, f32[2,2]{1,0:T(2,128)S(1)} %bitcast.23, ...), kind=kOutput, calls=%fused_computation.12 | convolution fusion | flops 69342208 | bytes 5949440 | tf_op jit(solution)/shard_map/xfcr,cl->xfrl/dot_general | solution.py:283
  64.1 0.0 collective-permute-done.7.below_ref
  64.1 0.0 collective-permute-done.6.above_ref
  64.1 0.0 copy-done
  64.1 0.0 copy-done.4
  64.1 0.0 copy-done.5
  64.1 32.8 %predict0.1 = (f32[2,16,256,512]{3,2,1,0:T(8,128)}, f32[8,128]{1,0:T(8,128)S(1)}) custom-call(s32[4]{0:T(128)S(1)} %copy-done.4, f32[5]{0:T(128)S(1)} %copy-done.5, f32[2,16,256,512]{3,2,1,0:T(8,128)} %wave_ref.5, f32[256,1]{1,0:T(8,128)S(1)} %copy.9.mask_ref, f32[2,8,48,512]{3,2,1,0:T(8,128)} %collective-permute-done.6.above_ref, ...), custom_call_target="tpu_custom_call" | custom-call | flops 8053063680 | bytes 20971520 | tf_op jit(solution)/shard_map/predict0/pallas_call | solution.py:120
  96.9 0.0 copy-start.2
  96.9 0.0 collective-permute-done.1.below_ref
  96.9 0.0 collective-permute-done.above_ref
  96.9 32.8 %predict8.1 = (f32[2,16,256,512]{3,2,1,0:T(8,128)}, f32[8,128]{1,0:T(8,128)S(1)}) custom-call(s32[4]{0:T(128)S(1)} %copy-done.4, f32[5]{0:T(128)S(1)} %copy-done.5, f32[2,16,256,512]{3,2,1,0:T(8,128)} %wave_ref.5, f32[256,1]{1,0:T(8,128)S(1)} %copy.9.mask_ref, f32[2,8,48,512]{3,2,1,0:T(8,128)S(1)} %collective-permute-done.above_ref, ...), custom_call_target="tpu_custom_call", output_to_operand_aliasing={{0}: (8, {})} | custom-call | flops 8053063680 | bytes 20971520 | tf_op jit(solution)/shard_map/predict8/pallas_call | solution.py:120
  129.7 0.0 copy-done.2
  129.7 0.0 copy-start.3
  129.7 0.6 copy-done.3
  130.3 14.6 %gains1.1.gain_ref = f32[8,128]{1,0:T(8,128)} custom-call(f32[8,128]{1,0:T(8,128)} %copy-done.2, f32[8,128]{1,0:T(8,128)} %copy-done.3), custom_call_target="tpu_custom_call" | custom-call | flops 1000 | bytes 8388608 | tf_op jit(solution)/shard_map/gains1/pallas_call | solution.py:199
  144.9 0.0 copy-start.1
  144.9 0.7 copy-done.1
  145.6 22.2 %subtract0.1 = f32[2,16,256,512]{3,2,1,0:T(8,128)} custom-call(f32[8,128]{1,0:T(8,128)S(1)} %copy-done.1, f32[2,16,256,512]{3,2,1,0:T(8,128)} %wave_ref.5, f32[2,16,256,512]{3,2,1,0:T(8,128)} %get-tuple-element.4.mult_ref), custom_call_target="tpu_custom_call" | custom-call | bytes 50331648 | tf_op jit(solution)/shard_map/subtract0/pallas_call | solution.py:238
  (1 shorter events, 0.0 us)
Async XLA Ops:
  7.7 56.4 %collective-permute-start.7 = (f32[2,8,48,512]{3,2,1,0:T(8,128)}, f32[2,8,48,512]{3,2,1,0:T(8,128)}, u32[]{:S(2)}, u32[]{:S(2)}) collective-permute-start(f32[2,8,48,512]{3,2,1,0:T(8,128)} %get-tuple-element.10), channel_id=1, source_target_pairs={{1,0},{2,1},{3,2},{4,3},{5,4},{6,5},{7,6},{9,8},{10,9},{11,10},{12... | collective-permute-start | bytes 4718600 | tf_op jit(solution)/shard_map/ppermute | solution.py:27
  8.9 55.1 %collective-permute-start.6 = (f32[2,8,48,512]{3,2,1,0:T(8,128)}, f32[2,8,48,512]{3,2,1,0:T(8,128)}, u32[]{:S(2)}, u32[]{:S(2)}) collective-permute-start(f32[2,8,48,512]{3,2,1,0:T(8,128)} %get-tuple-element.15), channel_id=1, source_target_pairs={{0,1},{1,2},{2,3},{3,4},{4,5},{5,6},{6,7},{8,9},{9,10},{10,11},{11... | collective-permute-start | bytes 4718600 | tf_op jit(solution)/shard_map/ppermute | solution.py:27
  17.4 12.5 %collective-permute-start.2 = (f32[2,16,2,256]{3,2,1,0:T(2,128)S(1)}, f32[2,16,2,256]{3,2,1,0:T(2,128)S(1)}, u32[]{:S(2)}, u32[]{:S(2)}) collective-permute-start(f32[2,16,2,256]{3,2,1,0:T(2,128)S(1)} %fusion.7), channel_id=1, source_target_pairs={{8,0},{16,8},{24,16},{9,1},{17,9},{25,17},{10,2},{18,10},{26,18},{... | collective-permute-start | bytes 196616 | tf_op jit(solution)/shard_map/ppermute | solution.py:27
  18.7 78.2 %collective-permute-start.1 = (f32[2,8,48,512]{3,2,1,0:T(8,128)}, f32[2,8,48,512]{3,2,1,0:T(8,128)S(1)}, u32[]{:S(2)}, u32[]{:S(2)}) collective-permute-start(f32[2,8,48,512]{3,2,1,0:T(8,128)} %get-tuple-element.11), channel_id=1, source_target_pairs={{1,0},{2,1},{3,2},{4,3},{5,4},{6,5},{7,6},{9,8},{10,9},{11,10},{12... | collective-permute-start | bytes 4718600 | tf_op jit(solution)/shard_map/ppermute | solution.py:27
  20.0 76.9 %collective-permute-start = (f32[2,8,48,512]{3,2,1,0:T(8,128)}, f32[2,8,48,512]{3,2,1,0:T(8,128)S(1)}, u32[]{:S(2)}, u32[]{:S(2)}) collective-permute-start(f32[2,8,48,512]{3,2,1,0:T(8,128)} %get-tuple-element.14), channel_id=1, source_target_pairs={{0,1},{1,2},{2,3},{3,4},{4,5},{5,6},{6,7},{8,9},{9,10},{10,11},{11... | collective-permute-start | bytes 4718600 | tf_op jit(solution)/shard_map/ppermute | solution.py:27
  29.8 6.6 %collective-permute-start.3 = (f32[2,16,2,256]{3,2,1,0:T(2,128)S(1)}, f32[2,16,2,256]{3,2,1,0:T(2,128)S(1)}, u32[]{:S(2)}, u32[]{:S(2)}) collective-permute-start(f32[2,16,2,256]{3,2,1,0:T(2,128)S(1)} %fusion.13), channel_id=1, source_target_pairs={{0,8},{8,16},{16,24},{1,9},{9,17},{17,25},{2,10},{10,18},{18,26},{... | collective-permute-start | bytes 196616 | tf_op jit(solution)/shard_map/ppermute | solution.py:27
  37.2 3.3 %collective-permute-start.4 = (f32[2,16,4,48]{3,2,1,0:T(4,128)S(1)}, f32[2,16,4,48]{3,2,1,0:T(4,128)S(1)}, u32[]{:S(2)}, u32[]{:S(2)}) collective-permute-start(f32[2,16,4,48]{3,2,1,0:T(4,128)S(1)} %get-tuple-element.16), channel_id=1, source_target_pairs={{0,1},{1,2},{2,3},{3,4},{4,5},{5,6},{6,7},{8,9},{9,10},{10,11},{11... | collective-permute-start | bytes 73736 | tf_op jit(solution)/shard_map/ppermute | solution.py:27
  40.5 12.1 %collective-permute-start.5 = (f32[2,16,4,48]{3,2,1,0:T(4,128)}, f32[2,16,4,48]{3,2,1,0:T(4,128)S(1)}, u32[]{:S(2)}, u32[]{:S(2)}) collective-permute-start(f32[2,16,4,48]{3,2,1,0:T(4,128)} %get-tuple-element.17), channel_id=1, source_target_pairs={{1,0},{2,1},{3,2},{4,3},{5,4},{6,5},{7,6},{9,8},{10,9},{11,10},{12... | collective-permute-start | bytes 73736 | tf_op jit(solution)/shard_map/ppermute | solution.py:27
  42.1 22.0 %copy-start = (f32[2,256,1024]{2,1,0:T(8,128)S(1)}, f32[2,256,1024]{2,1,0:T(8,128)}, u32[]{:S(2)}) copy-start(f32[2,256,1024]{2,1,0:T(8,128)} %band_ref.3) | copy-start | bytes 6291460
  42.1 22.0 %copy-start.4 = (s32[4]{0:T(128)S(1)}, s32[4]{0:T(128)}, u32[]{:S(2)}) copy-start(s32[4]{0:T(128)} %shift_ref.3) | copy-start | bytes 52
  42.1 22.0 %copy-start.5 = (f32[5]{0:T(128)S(1)}, f32[5]{0:T(128)}, u32[]{:S(2)}) copy-start(f32[5]{0:T(128)} %taper_ref.3) | copy-start | bytes 64
  96.9 32.8 %copy-start.2 = (f32[8,128]{1,0:T(8,128)}, f32[8,128]{1,0:T(8,128)S(1)}, u32[]{:S(2)}) copy-start(f32[8,128]{1,0:T(8,128)S(1)} %get-tuple-element.8.refs_0_) | copy-start | bytes 12292
  129.7 0.6 copy-start.3
  144.9 0.7 copy-start.1
where the time goes:
time: 168 us
  Pallas kernels  102 us (61%)
  matrix products  21.3 us (13%)
  starting transfers between devices  20.6 us (12%)
  waiting for transfers between devices  13.4 us (8%)
  other arithmetic  7.68 us (5%)
    pallas_call x2, Pallas kernels, predict(): pl.pallas_call(functools.partial(predict_kernel, first), grid=(count,), i...  65.6 us
    pallas_call x1, Pallas kernels, subtract(): pl.pallas_call(functools.partial(subtract_kernel, first), grid=(count,),...  22.2 us
    ppermute x8, starting transfers between devices, shifted(): return lax.ppermute(cells, axis, pairs)  20.6 us
    pallas_call x1, Pallas kernels, gains(): pl.pallas_call(functools.partial(gain_kernel, axes), in_specs=[pl.BlockSp...  14.6 us
    ppermute x8, waiting for transfers between devices, shifted(): return lax.ppermute(cells, axis, pairs)  13.4 us
    dot_general x1, matrix products, per_device(): side = turn('xfcr,cl->xfrl', sides, place)  11.4 us
    mul x1, other arithmetic, per_device(): head = part[:, :, :HALO] * mask[None, None, :HALO, None]  6.27 us
    dot_general x1, matrix products, per_device(): turn('cl,xfrl->xfcr', jnp.roll(pick, -SHALF, 1), wavefield[..., shots - L...  5.66 us
  transfers between devices with their start and end apart: 8, of which 3 were waited for; matrix products, arithmetic and copies ran while one was open for 13% of the time, Pallas kernels for 20%

commit v1 on v0

v1 whole, which is shorter than its diff:
```python
import functools

import jax
import jax.numpy as jnp
from jax import lax
from jax.experimental import pallas as pl
from jax.experimental.pallas import tpu as pltpu
from jax.sharding import PartitionSpec as P

APER = 64
SHIFT = 16
BLOCK = 64
HALF = BLOCK // 2
SHALF = 2
LANES = 128
DEPTH = 128
HALO = APER // 2 + SHIFT
FIRST = 2
STRIP = 16
SLOTS = 8
MESH = pl.DeviceIdType.MESH


def split(cells):
    high = cells.astype(jnp.bfloat16)
    low = (cells - high.astype(jnp.float32)).astype(jnp.bfloat16)
    return high, low


def forward_kernel(axes, shift_ref, taper_ref, mask_ref, wave_hbm, band_hbm, *refs):
    wave_ref, mult_ref, gain_ref = refs[:3]
    (
        band_ref, weight_ref, turn_ref, high_ref, low_ref, above_ref, below_ref, edge_ref, next_ref, prev_ref, corner_ref, masks_ref,
        data_ref, pred_ref, mine_ref, plane_ref, space_ref,
        load_sem, band_sem, send_up, recv_up, send_down, recv_down, send_mask, recv_mask,
        send_edge, recv_edge, send_corner, recv_corner, own_sem, send_a, recv_a, send_b, recv_b,
    ) = refs[3:]
    (slow, slow_count), (fast, fast_count) = axes
    slow_me, fast_me = lax.axis_index(slow), lax.axis_index(fast)
    _, slices, receivers, shots = wave_ref.shape
    blocks = receivers // BLOCK
    has_above, has_below = fast_me > 0, fast_me < fast_count - 1
    has_prev, has_next = slow_me > 0, slow_me < slow_count - 1

    def slow_peer(d):
        return {slow: lax.rem(slow_me + d, slow_count)}

    def fast_peer(d):
        return {fast: lax.rem(fast_me + d, fast_count)}

    corners = []
    for i, (down, right) in enumerate([(1, 1), (1, -1), (-1, 1), (-1, -1)]):
        there = (has_below if down > 0 else has_above) & (has_next if right > 0 else has_prev)
        came = (has_above if down > 0 else has_below) & (has_prev if right > 0 else has_next)
        peer = {fast: fast_me + down, slow: slow_me + right}
        rows = pl.ds(receivers - HALO if down > 0 else 0, HALO)
        corners.append((i, there, came, peer, rows))

    def load(f):
        return pltpu.make_async_copy(wave_hbm.at[:, f], wave_ref.at[:, f], load_sem.at[f])

    def up(f):
        return pltpu.make_async_remote_copy(
            src_ref=wave_hbm.at[:, f, pl.ds(receivers - HALO, HALO)], dst_ref=above_ref.at[f],
            send_sem=send_up.at[f], recv_sem=recv_up.at[f],
            device_id={fast: fast_me + 1}, device_id_type=MESH,
        )

    def down(f):
        return pltpu.make_async_remote_copy(
            src_ref=wave_hbm.at[:, f, pl.ds(0, HALO)], dst_ref=below_ref.at[f],
            send_sem=send_down.at[f], recv_sem=recv_down.at[f],
            device_id={fast: fast_me - 1}, device_id_type=MESH,
        )

    def mask_copy(i):
        return pltpu.make_async_remote_copy(
            src_ref=mask_ref.at[pl.ds(0 if i else receivers - HALO, HALO)], dst_ref=masks_ref.at[i],
            send_sem=send_mask.at[i], recv_sem=recv_mask.at[i],
            device_id={fast: fast_me - 1 if i else fast_me + 1}, device_id_type=MESH,
        )

    def edge_copy(i):
        return pltpu.make_async_remote_copy(
            src_ref=edge_ref, dst_ref=next_ref if i else prev_ref,
            send_sem=send_edge.at[i], recv_sem=recv_edge.at[i],
            device_id={slow: slow_me - 1 if i else slow_me + 1}, device_id_type=MESH,
        )

    def corner_copy(i, peer, rows):
        return pltpu.make_async_remote_copy(
            src_ref=edge_ref.at[rows], dst_ref=corner_ref.at[i],
            send_sem=send_corner.at[i], recv_sem=recv_corner.at[i],
            device_id=peer, device_id_type=MESH,
        )

    def send_halos(f):
        @pl.when(has_below)
        def _():
            up(f).start()

        @pl.when(has_above)
        def _():
            down(f).start()

    barrier = pltpu.get_barrier_semaphore()
    for d in range(1, slow_count):
        pl.semaphore_signal(barrier, inc=1, device_id=slow_peer(d), device_id_type=MESH)
    for d in range(1, fast_count):
        pl.semaphore_signal(barrier, inc=1, device_id=fast_peer(d), device_id_type=MESH)
    for i, there, came, peer, rows in corners:
        @pl.when(there)
        def _():
            pl.semaphore_signal(barrier, inc=1, device_id=peer, device_id_type=MESH)

    @pl.loop(0, slices)
    def _(f):
        load(f).start()

    band_copy = pltpu.make_async_copy(band_hbm, band_ref, band_sem)
    band_copy.start()

    zeros = jnp.zeros((STRIP, shots), jnp.bfloat16)
    for x in range(2):
        @pl.loop(0, high_ref.shape[1] // STRIP)
        def _(i):
            rows = pl.ds(pl.multiple_of(i * STRIP, STRIP), STRIP)
            high_ref[x, rows, :] = zeros
            low_ref[x, rows, :] = zeros

    @pl.when(jnp.logical_not(has_prev))
    def _():
        prev_ref[...] = jnp.zeros_like(prev_ref)

    @pl.when(jnp.logical_not(has_next))
    def _():
        next_ref[...] = jnp.zeros_like(next_ref)

    for i, there, came, peer, rows in corners:
        @pl.when(jnp.logical_not(came))
        def _():
            corner_ref[i] = jnp.zeros(corner_ref.shape[1:], jnp.float32)

    edge_ref[...] = jnp.zeros_like(edge_ref)
    greeted = sum(there.astype(jnp.int32) for _, there, *_ in corners)
    pl.semaphore_wait(barrier, slow_count + fast_count - 2 + greeted)

    @pl.when(has_below)
    def _():
        mask_copy(0).start()

    @pl.when(has_above)
    def _():
        mask_copy(1).start()

    for f in range(FIRST):
        send_halos(f)

    lane = lax.broadcasted_iota(jnp.int32, (BLOCK, LANES), 1)

    @pl.loop(0, slices)
    def _(f):
        load(f).wait()
        for b in range(blocks):
            rows = pl.ds(b * BLOCK, BLOCK)
            edges = edge_ref[rows, :]
            for x in range(2):
                place = 4 * f + 2 * x
                ours = (lane >= place) & (lane < place + 2)
                edges = jnp.where(ours, pltpu.roll(wave_ref[x, f, rows, :LANES], place, 1), edges)
                place = place + LANES // 2
                ours = (lane >= place) & (lane < place + 2)
                turned = pltpu.roll(wave_ref[x, f, rows, shots - LANES :], lax.rem(place + 2, LANES), 1)
                edges = jnp.where(ours, turned, edges)
            edge_ref[rows, :] = edges

    @pl.when(has_next)
    def _():
        edge_copy(0).start()

    @pl.when(has_prev)
    def _():
        edge_copy(1).start()

    for i, there, came, peer, rows in corners:
        @pl.when(there)
        def _():
            corner_copy(i, peer, rows).start()

    @pl.loop(FIRST, slices)
    def _(f):
        send_halos(f)

    source = lax.broadcasted_iota(jnp.int32, (2 * LANES, LANES), 0)
    source = jnp.where(source < LANES, source, jnp.where(source < LANES + LANES // 2, source, source - 2 * LANES))
    offset = source - lax.broadcasted_iota(jnp.int32, (2 * LANES, LANES), 1) + SHALF
    turn = jnp.zeros((2 * LANES, LANES), jnp.float32)
    for u in range(2 * SHALF + 1):
        turn = jnp.where(offset == u, taper_ref[u], turn)
    turn = jnp.concatenate(split(turn), axis=1)
    for i in range(2):
        turn_ref[2 * i * LANES : 2 * (i + 1) * LANES, :] = turn

    column = lax.broadcasted_iota(jnp.int32, (BLOCK, LANES), 1)

    def prepare(f):
        odd, slot = lax.rem(f, 2), lax.rem(f, 2)
        live = (column // APER) == odd
        lanes = pl.ds(pl.multiple_of(f // 2 * LANES, LANES), LANES)
        for block in range(blocks):
            for x in range(2):
                cells = jnp.where(live, band_ref[x, block * BLOCK : (block + 1) * BLOCK, lanes], 0.0)
                cells = pltpu.roll(cells, shift_ref[block] + SHIFT + APER * odd, 1)
                for h in range(2):
                    taps = pltpu.roll(cells[h * HALF : (h + 1) * HALF], 0, 1, stride=1, stride_axis=0)
                    weight_ref[slot, 2 * block + h, 0, x], weight_ref[slot, 2 * block + h, 1, x] = split(taps)

    band_copy.wait()
    prepare(0)

    @pl.when(has_above)
    def _():
        mask_copy(0).wait_recv()

    @pl.when(has_below)
    def _():
        mask_copy(1).wait_recv()

    @pl.when(has_prev)
    def _():
        edge_copy(0).wait_recv()

    @pl.when(has_next)
    def _():
        edge_copy(1).wait_recv()

    for i, there, came, peer, rows in corners:
        @pl.when(came)
        def _():
            corner_copy(i, peer, rows).wait_recv()

    def stage(x, f, wave, mask, after, before, at):
        count = wave.shape[0]
        tile = lax.broadcasted_iota(jnp.int32, (count, LANES), 1) < LANES // 2
        place = 4 * f + 2 * x
        after = pltpu.roll(after, lax.rem(LANES - place, LANES), 1)
        before = pltpu.roll(before, lax.rem(LANES + LANES // 2 - place - 2, LANES), 1)
        outside = split(jnp.where(tile, after, before) * mask)
        inside = [split(wave[:, i * LANES : (i + 1) * LANES] * mask) for i in range(shots // LANES)]
        cells = [outside, *inside, outside]
        parts = []
        for part in range(2):
            rows = []
            for i in range(shots // LANES):
                around = jnp.where(tile, cells[i + 2][part], cells[i][part])
                rows.append(jnp.concatenate([cells[i + 1][part], around], axis=1))
            parts.append(jnp.concatenate(rows, axis=0))
        both = jnp.dot(jnp.concatenate(parts, axis=1), turn_ref[...], preferred_element_type=jnp.float32)
        high, low = split(both[:, :LANES] + both[:, LANES:])
        rows = pl.ds(at, count)
        for i in range(shots // LANES):
            lanes = pl.ds(i * LANES, LANES)
            high_ref[x, rows, lanes] = high[i * count : (i + 1) * count]
            low_ref[x, rows, lanes] = low[i * count : (i + 1) * count]

    def predict(f, block):
        slot = lax.rem(f, 2)
        total = jnp.zeros((8, shots), jnp.float32)
        for h in range(2):
            half = 2 * block + h
            base = half * HALF
            parts = []
            for part in range(2):
                real, imag = weight_ref[slot, half, part, 0], weight_ref[slot, half, part, 1]
                parts.append(jnp.concatenate([real, -imag], axis=1))
                parts.append(jnp.concatenate([imag, real], axis=1))
            window = pl.ds(base, DEPTH)
            high = jnp.concatenate([high_ref[x, window, :] for x in range(2)], axis=0)
            low = jnp.concatenate([low_ref[x, window, :] for x in range(2)], axis=0)
            upper = jnp.dot(jnp.concatenate(parts, axis=0), high, preferred_element_type=jnp.float32)
            lower = jnp.dot(jnp.concatenate(parts[:2], axis=0), low, preferred_element_type=jnp.float32)
            pred = upper[:BLOCK] + (upper[BLOCK:] + lower)
            for x in range(2):
                mult_ref[x, f, pl.ds(base, HALF), :] = pred[x * HALF : (x + 1) * HALF]
            total = total + jnp.sum((pred * pred).reshape(-1, 8, shots), axis=0)
        return total

    def lanes_of(total):
        return sum(total[:, i * LANES : (i + 1) * LANES] for i in range(shots // LANES))

    @pl.loop(0, slices)
    def _(f):
        def own(i, data):
            rows = pl.ds(pl.multiple_of(i * BLOCK, BLOCK), BLOCK)
            at = pl.multiple_of(i * BLOCK + HALO, STRIP)
            for x in range(2):
                wave = wave_ref[x, f, rows, :]
                stage(x, f, wave, mask_ref[rows, :], next_ref[rows, :], prev_ref[rows, :], at)
                data = data + lanes_of(jnp.sum((wave * wave).reshape(-1, 8, shots), axis=0))
            return data

        data_ref[f] = lax.fori_loop(0, blocks, own, jnp.zeros((8, LANES), jnp.float32), unroll=True)

        prepare(jnp.minimum(f + 1, slices - 1))
        total = jnp.zeros((8, shots), jnp.float32)
        for block in range(1, blocks - 1):
            total = total + predict(f, block)

        @pl.when(has_above)
        def _():
            up(f).wait_recv()
            for x in range(2):
                stage(x, f, above_ref[f, x], masks_ref[0], corner_ref[1], corner_ref[0], 0)

        @pl.when(has_below)
        def _():
            down(f).wait_recv()
            for x in range(2):
                stage(x, f, below_ref[f, x], masks_ref[1], corner_ref[3], corner_ref[2], HALO + receivers)

        for block in sorted({0, blocks - 1}):
            total = total + predict(f, block)
        pred_ref[f] = lanes_of(total)

    row = lax.broadcasted_iota(jnp.int32, (8, LANES), 0)
    col = lax.broadcasted_iota(jnp.int32, (8, LANES), 1)
    mine = jnp.zeros((8, LANES), jnp.float32)
    for f in range(slices):
        mine = jnp.where((row == 0) & (col == f), jnp.sum(data_ref[f]), mine)
        mine = jnp.where((row == 1) & (col == f), jnp.sum(pred_ref[f]), mine)
    mine_ref[...] = mine

    own = pltpu.make_async_copy(mine_ref, plane_ref.at[0], own_sem)
    own.start()
    copies = []
    for d in range(1, slow_count):
        copy = pltpu.make_async_remote_copy(
            src_ref=mine_ref, dst_ref=plane_ref.at[d], send_sem=send_a.at[d], recv_sem=recv_a.at[d],
            device_id=slow_peer(d), device_id_type=MESH,
        )
        copy.start()
        copies.append(copy)
    own.wait()
    for copy in copies:
        copy.wait()
    copies = []
    for d in range(1, fast_count):
        copy = pltpu.make_async_remote_copy(
            src_ref=plane_ref, dst_ref=space_ref.at[d - 1], send_sem=send_b.at[d], recv_sem=recv_b.at[d],
            device_id=fast_peer(d), device_id_type=MESH,
        )
        copy.start()
        copies.append(copy)
    total = jnp.sum(plane_ref[...], axis=0)
    for copy in copies:
        copy.wait()
    for d in range(fast_count - 1):
        total = total + jnp.sum(space_ref[d], axis=0)
    data = jnp.broadcast_to(total[0:1], total.shape)
    pred = jnp.broadcast_to(total[1:2], total.shape)
    gain_ref[...] = jnp.sqrt((data + 1e-06) / (pred + 1e-06))

    @pl.when(has_below)
    def _():
        mask_copy(0).wait_send()

        @pl.loop(0, slices)
        def _(f):
            up(f).wait_send()

    @pl.when(has_above)
    def _():
        mask_copy(1).wait_send()

        @pl.loop(0, slices)
        def _(f):
            down(f).wait_send()

    @pl.when(has_next)
    def _():
        edge_copy(0).wait_send()

    @pl.when(has_prev)
    def _():
        edge_copy(1).wait_send()

    for i, there, came, peer, rows in corners:
        @pl.when(there)
        def _():
            corner_copy(i, peer, rows).wait_send()


def forward(axes, wave, band, shift, mask, taper):
    _, slices, receivers, shots = wave.shape
    slow_count, fast_count = axes[0][1], axes[1][1]
    tall = receivers + DEPTH - HALF
    dma = pltpu.SemaphoreType.DMA
    whole = pl.BlockSpec(memory_space=pltpu.VMEM)
    scalars = pl.BlockSpec(memory_space=pltpu.SMEM)
    hbm = pl.BlockSpec(memory_space=pltpu.HBM)
    return pl.pallas_call(
        functools.partial(forward_kernel, axes),
        in_specs=[scalars, scalars, whole, hbm, hbm],
        out_specs=[whole, whole, whole],
        out_shape=[
            jax.ShapeDtypeStruct(wave.shape, jnp.float32),
            jax.ShapeDtypeStruct(wave.shape, jnp.float32),
            jax.ShapeDtypeStruct((8, LANES), jnp.float32),
        ],
        scratch_shapes=[
            pltpu.VMEM(band.shape, jnp.float32),
            pltpu.VMEM((2, receivers // HALF, 2, 2, HALF, DEPTH), jnp.bfloat16),
            pltpu.VMEM((4 * LANES, 2 * LANES), jnp.bfloat16),
            pltpu.VMEM((2, tall, shots), jnp.bfloat16),
            pltpu.VMEM((2, tall, shots), jnp.bfloat16),
            pltpu.VMEM((slices, 2, HALO, shots), jnp.float32),
            pltpu.VMEM((slices, 2, HALO, shots), jnp.float32),
            pltpu.VMEM((receivers, LANES), jnp.float32),
            pltpu.VMEM((receivers, LANES), jnp.float32),
            pltpu.VMEM((receivers, LANES), jnp.float32),
            pltpu.VMEM((4, HALO, LANES), jnp.float32),
            pltpu.VMEM((2, HALO, LANES), jnp.float32),
            pltpu.VMEM((slices, 8, LANES), jnp.float32),
            pltpu.VMEM((slices, 8, LANES), jnp.float32),
            pltpu.VMEM((8, LANES), jnp.float32),
            pltpu.VMEM((slow_count, 8, LANES), jnp.float32),
            pltpu.VMEM((fast_count - 1, slow_count, 8, LANES), jnp.float32),
            dma((slices,)), dma, dma((slices,)), dma((slices,)), dma((slices,)), dma((slices,)),
            dma((2,)), dma((2,)), dma((2,)), dma((2,)), dma((4,)), dma((4,)), dma,
            dma((slow_count,)), dma((slow_count,)), dma((fast_count,)), dma((fast_count,)),
        ],
        cost_estimate=pl.CostEstimate(flops=2**33, bytes_accessed=wave.size * 8, transcendentals=0),
        compiler_params=pltpu.CompilerParams(
            collective_id=1, has_side_effects=True, vmem_limit_bytes=12 * 2**20
        ),
        name="forward",
    )(shift, taper, mask, wave, band)


def finish_kernel(gain_ref, wave_ref, mult_ref, mult_hbm, prim_hbm, prim_ref, mult_sem, prim_sem):
    slices = wave_ref.shape[1]
    slots = prim_ref.shape[0]

    def mult_copy(f):
        return pltpu.make_async_copy(mult_ref.at[:, f], mult_hbm.at[:, f], mult_sem.at[f])

    def prim_copy(f):
        return pltpu.make_async_copy(prim_ref.at[lax.rem(f, slots)], prim_hbm.at[:, f], prim_sem.at[f])

    col = lax.broadcasted_iota(jnp.int32, (1, LANES), 1)

    @pl.loop(0, slices)
    def _(f):
        mult_copy(f).start()
        gain = jnp.sum(jnp.where(col == f, gain_ref[0:1, :], 0.0))

        @pl.when(f >= slots)
        def _():
            prim_copy(f - slots).wait()

        for x in range(2):
            for r in range(0, wave_ref.shape[2], BLOCK):
                rows = pl.ds(r, BLOCK)
                prim_ref[lax.rem(f, slots), x, rows, :] = wave_ref[x, f, rows, :] - gain * mult_ref[x, f, rows, :]
        prim_copy(f).start()

    @pl.loop(0, slices)
    def _(f):
        mult_copy(f).wait()

    @pl.loop(max(slices - slots, 0), slices)
    def _(f):
        prim_copy(f).wait()


def finish(gain, wave, mult):
    slices = wave.shape[1]
    whole = pl.BlockSpec(memory_space=pltpu.VMEM)
    hbm = pl.BlockSpec(memory_space=pl.ANY)
    return pl.pallas_call(
        finish_kernel,
        in_specs=[whole, whole, whole],
        out_specs=[hbm, hbm],
        out_shape=[jax.ShapeDtypeStruct(wave.shape, jnp.float32)] * 2,
        scratch_shapes=[
            pltpu.VMEM((min(SLOTS, slices), 2, *wave.shape[2:]), jnp.float32),
            pltpu.SemaphoreType.DMA((slices,)),
            pltpu.SemaphoreType.DMA((slices,)),
        ],
        cost_estimate=pl.CostEstimate(flops=wave.size * 2, bytes_accessed=wave.size * 8, transcendentals=0),
        compiler_params=pltpu.CompilerParams(vmem_limit_bytes=12 * 2**20),
        name="finish",
    )(gain, wave, mult)


def per_device(wavefield, surface_band, band_shift, trace_mask, shot_taper):
    receivers = wavefield.shape[2]
    axes = (("src", lax.axis_size("src")), ("rcv", lax.axis_size("rcv")))
    mask = jnp.broadcast_to(trace_mask.astype(jnp.float32)[:, None], (receivers, LANES))
    wave, mult, gain = forward(axes, wavefield, surface_band, band_shift, mask, shot_taper)
    return tuple(finish(gain, wave, mult))


def solution(mesh):
    in_specs = (P(None, None, "rcv", "src"), P(None, "rcv", None), P("rcv"), P("rcv"), P())
    out_specs = (P(None, None, "rcv", "src"), P(None, None, "rcv", "src"))
    return jax.shard_map(
        per_device, mesh=mesh, in_specs=in_specs, out_specs=out_specs, check_vma=False
    )
```

time: 168 us -> 78.8 us (0.47)
  Pallas kernels: 102 us -> 74.3 us
  matrix products: 21.3 us -> 0 us
  starting transfers between devices: 20.6 us -> 0 us
  waiting for transfers between devices: 13.4 us -> 0 us
  other arithmetic: 7.68 us -> 0.68 us
    pallas_call x4 -> x2, Pallas kernels: 102 us -> 74.3 us  [the longest x1 63.1 us: forward(): pl.pallas_call(functools.partial(forward_kernel, axes), in_specs=[scalars...]
    dot_general x3 -> x0, matrix products: 21.3 us -> none  [the longest x1 11.4 us: per_device(): side = turn('xfcr,cl->xfrl', sides, place)]
    ppermute x8 -> x0, starting transfers between devices: 20.6 us -> none  [shifted(): return lax.ppermute(cells, axis, pairs)]
    ppermute x8 -> x0, waiting for transfers between devices: 13.4 us -> none  [shifted(): return lax.ppermute(cells, axis, pairs)]
    mul x1 -> x0, other arithmetic: 6.27 us -> none  [per_device(): head = part[:, :, :HALO] * mask[None, None, :HALO, None]]
  transfers between devices with their start and end apart: 8 -> 0, of which waited for: 3 -> 0; matrix products, arithmetic and copies ran while one was open for 13% -> 0% of each run, Pallas kernels for 20% -> 0%
where the time goes in v1:
time: 78.8 us; the launch traced here: 78.6 us
  Pallas kernels  74.3 us (94%)
  local copies, waits for them, and re-layouts  2.99 us (4%)
    pallas_call x1, Pallas kernels, forward(): pl.pallas_call(functools.partial(forward_kernel, axes), in_specs=[scalars...  63.1 us
    pallas_call x1, Pallas kernels, finish(): pl.pallas_call(finish_kernel, in_specs=[whole, whole, whole], out_specs=[...  11.2 us
    unnamed x6, local copies, waits for them, and re-layouts  2.9 us

profile of v1, /device:TPU:0, one launch (start us, length us, event | category | flops | bytes accessed | tf_op | source)
XLA Modules:
  0.0 78.6 jit_solution(8819743359275901722)
XLA Ops:
  0.6 0.7 convert_element_type.3
  1.3 0.1 broadcast_in_dim.2.mask_ref
  1.4 0.0 copy-start
  1.4 1.6 %copy-done = f32[2,256,1024]{2,1,0:T(8,128)S(1)} copy-done((f32[2,256,1024]{2,1,0:T(8,128)S(1)}, f32[2,256,1024]{2,1,0:T(8,128)}, u32[]{:S(2)}) %copy-start) | copy-done | bytes 2097176
  3.0 0.0 copy-start.1
  3.0 0.7 copy-done.1
  3.7 0.0 copy-start.2
  3.7 0.7 copy-done.2
  4.3 63.1 %forward.1 = (f32[2,16,256,512]{3,2,1,0:T(8,128)S(1)}, f32[2,16,256,512]{3,2,1,0:T(8,128)S(1)}, f32[8,128]{1,0:T(8,128)S(1)}) custom-call(s32[4]{0:T(128)S(1)} %copy-done.1, f32[5]{0:T(128)S(1)} %copy-done.2, f32[256,128]{1,0:T(8,128)S(1)} %broadcast_in_dim.2.mask_ref, f32[2,16,256,512]{3,2,1,0:T(8,128)} %wave_hbm.1, f32[2,256,1024]{2,1,0:T(8,128)S(1)} %copy-done), custom_call_target="tpu_custom_call" | custom-call | flops 8589934592 | bytes 33554432 | tf_op jit(solution)/shard_map/forward/pallas_call | solution.py:401
  67.5 11.2 %finish.1 = (f32[2,16,256,512]{3,2,1,0:T(8,128)}, f32[2,16,256,512]{3,2,1,0:T(8,128)}) custom-call(f32[8,128]{1,0:T(8,128)S(1)} %get-tuple-element.5.gain_ref, f32[2,16,256,512]{3,2,1,0:T(8,128)S(1)} %get-tuple-element.6.wave_ref, f32[2,16,256,512]{3,2,1,0:T(8,128)S(1)} %get-tuple-element.7.mult_ref), custom_call_target="tpu_custom_call" | custom-call | flops 8388608 | bytes 33554432 | tf_op jit(solution)/shard_map/finish/pallas_call | solution.py:480
Async XLA Ops:
  1.4 1.6 %copy-start = (f32[2,256,1024]{2,1,0:T(8,128)S(1)}, f32[2,256,1024]{2,1,0:T(8,128)}, u32[]{:S(2)}) copy-start(f32[2,256,1024]{2,1,0:T(8,128)} %band_hbm.1) | copy-start | bytes 6291460
  3.0 0.7 copy-start.1
  3.7 0.7 copy-start.2

commit v2 on v1

v2 whole, which is shorter than its diff:
```python
import functools

import jax
import jax.numpy as jnp
from jax import lax
from jax.experimental import pallas as pl
from jax.experimental.pallas import tpu as pltpu
from jax.sharding import PartitionSpec as P

APER = 64
SHIFT = 16
BLOCK = 64
HALF = BLOCK // 2
SHALF = 2
LANES = 128
DEPTH = 128
HALO = APER // 2 + SHIFT
FIRST = 3
GROUPS = 2
STRIP = 16
SLOTS = 8
MESH = pl.DeviceIdType.MESH


def split(cells):
    high = cells.astype(jnp.bfloat16)
    low = (cells - high.astype(jnp.float32)).astype(jnp.bfloat16)
    return high, low


def forward_kernel(axes, shift_hbm, taper_hbm, live_hbm, wave_hbm, band_hbm, *refs):
    wave_ref, mult_ref, gain_ref = refs[:3]
    (
        shift_ref, taper_ref, live_ref, mask_ref, band_ref, turn_ref,
        even_weight, odd_weight, even_high, odd_high, even_low, odd_low, above_ref, below_ref, edge_ref, next_ref, prev_ref, ends_ref, corner_ref, masks_ref,
        data_ref, inner_ref, outer_ref, mine_ref, plane_ref, space_ref,
        load_sem, small_sem, send_up, recv_up, send_down, recv_down, send_mask, recv_mask,
        send_edge, recv_edge, send_corner, recv_corner, send_a, recv_a, send_b, recv_b,
    ) = refs[3:]
    (slow, slow_count), (fast, fast_count) = axes
    slow_me, fast_me = lax.axis_index(slow), lax.axis_index(fast)
    _, slices, receivers, shots = wave_ref.shape
    blocks, group = receivers // BLOCK, slices // GROUPS
    share = 4 * group
    quarters = LANES // share
    has_above, has_below = fast_me > 0, fast_me < fast_count - 1
    has_prev, has_next = slow_me > 0, slow_me < slow_count - 1
    direct = slow_count * fast_count <= 32

    def peer_of(a, b):
        return {slow: lax.rem(slow_me + a, slow_count), fast: lax.rem(fast_me + b, fast_count)}

    corners = []
    for i, (down, right) in enumerate([(1, 1), (1, -1), (-1, 1), (-1, -1)]):
        there = (has_below if down > 0 else has_above) & (has_next if right > 0 else has_prev)
        came = (has_above if down > 0 else has_below) & (has_prev if right > 0 else has_next)
        corners.append((i, there, came, {fast: fast_me + down, slow: slow_me + right}, 0 if down > 0 else 1))

    def load(f):
        return pltpu.make_async_copy(wave_hbm.at[:, f], wave_ref.at[:, f], load_sem.at[f])

    def up(f):
        return pltpu.make_async_remote_copy(
            src_ref=wave_hbm.at[:, f, pl.ds(receivers - HALO, HALO)], dst_ref=above_ref.at[f],
            send_sem=send_up.at[f], recv_sem=recv_up.at[f],
            device_id={fast: fast_me + 1}, device_id_type=MESH,
        )

    def down(f):
        return pltpu.make_async_remote_copy(
            src_ref=wave_hbm.at[:, f, pl.ds(0, HALO)], dst_ref=below_ref.at[f],
            send_sem=send_down.at[f], recv_sem=recv_down.at[f],
            device_id={fast: fast_me - 1}, device_id_type=MESH,
        )

    def mask_copy(i):
        return pltpu.make_async_remote_copy(
            src_ref=mask_ref.at[pl.ds(0 if i else receivers - HALO, HALO)], dst_ref=masks_ref.at[i],
            send_sem=send_mask.at[i], recv_sem=recv_mask.at[i],
            device_id={fast: fast_me - 1 if i else fast_me + 1}, device_id_type=MESH,
        )

    def edge_copy(g, i):
        return pltpu.make_async_remote_copy(
            src_ref=edge_ref.at[g, 1 - i], dst_ref=next_ref.at[g] if i else prev_ref.at[g],
            send_sem=send_edge.at[g, i], recv_sem=recv_edge.at[g, i],
            device_id={slow: slow_me - 1 if i else slow_me + 1}, device_id_type=MESH,
        )

    def corner_copy(i, peer, end):
        return pltpu.make_async_remote_copy(
            src_ref=ends_ref.at[end], dst_ref=corner_ref.at[i],
            send_sem=send_corner.at[i], recv_sem=recv_corner.at[i],
            device_id=peer, device_id_type=MESH,
        )

    def send_halos(f):
        @pl.when(has_below)
        def _():
            up(f).start()

        @pl.when(has_above)
        def _():
            down(f).start()

    small = [
        pltpu.make_async_copy(a, b, small_sem.at[i])
        for i, (a, b) in enumerate(
            [(live_hbm, live_ref), (taper_hbm, taper_ref), (shift_hbm, shift_ref), (band_hbm, band_ref)]
        )
    ]
    for copy in small[:3]:
        copy.start()
    barrier = pltpu.get_barrier_semaphore()
    if direct:
        greeted = slow_count * fast_count - 1
        for a in range(slow_count):
            for b in range(fast_count):
                if a or b:
                    pl.semaphore_signal(barrier, inc=1, device_id=peer_of(a, b), device_id_type=MESH)
    else:
        greeted = slow_count + fast_count - 2 + sum(there.astype(jnp.int32) for _, there, *_ in corners)
        for a in range(1, slow_count):
            pl.semaphore_signal(barrier, inc=1, device_id=peer_of(a, 0), device_id_type=MESH)
        for b in range(1, fast_count):
            pl.semaphore_signal(barrier, inc=1, device_id=peer_of(0, b), device_id_type=MESH)
        for i, there, came, peer, end in corners:
            @pl.when(there)
            def _():
                pl.semaphore_signal(barrier, inc=1, device_id=peer, device_id_type=MESH)

    small[3].start()

    @pl.loop(0, slices)
    def _(f):
        load(f).start()

    small[0].wait()
    line = lax.broadcasted_iota(jnp.int32, (8, LANES), 0)

    @pl.loop(0, receivers // 8)
    def _(i):
        cells = jnp.zeros((8, LANES), jnp.float32)
        for r in range(8):
            cells = jnp.where(line == r, live_ref[i * 8 + r].astype(jnp.float32), cells)
        mask_ref[pl.ds(pl.multiple_of(i * 8, 8), 8), :] = cells

    small[1].wait()
    small[2].wait()

    source = lax.broadcasted_iota(jnp.int32, (2 * LANES, LANES), 0)
    source = jnp.where(source < LANES, source, jnp.where(source < LANES + LANES // 2, source, source - 2 * LANES))
    offset = source - lax.broadcasted_iota(jnp.int32, (2 * LANES, LANES), 1) + SHALF
    turn = jnp.zeros((2 * LANES, LANES), jnp.float32)
    for u in range(2 * SHALF + 1):
        turn = jnp.where(offset == u, taper_ref[u], turn)
    turn = jnp.concatenate(split(turn), axis=1)
    for i in range(2):
        turn_ref[2 * i * LANES : 2 * (i + 1) * LANES, :] = turn

    rows_refs, weight_refs = ((even_high, even_low), (odd_high, odd_low)), (even_weight, odd_weight)
    zeros = jnp.zeros((STRIP, shots), jnp.bfloat16)
    for x in range(2):
        @pl.loop(0, even_high.shape[1] // STRIP)
        def _(i):
            rows = pl.ds(pl.multiple_of(i * STRIP, STRIP), STRIP)
            for ref in (even_high, odd_high, even_low, odd_low):
                ref[x, rows, :] = zeros

    for there, ref in ((has_prev, prev_ref), (has_next, next_ref)):
        @pl.when(jnp.logical_not(there))
        def _():
            ref[...] = jnp.zeros_like(ref)

    for i, there, came, peer, end in corners:
        @pl.when(jnp.logical_not(came))
        def _():
            corner_ref[i] = jnp.zeros(corner_ref.shape[1:], jnp.float32)

    for i, (there, ref) in enumerate(((has_above, above_ref), (has_below, below_ref))):
        @pl.when(jnp.logical_not(there))
        def _():
            masks_ref[i] = jnp.zeros(masks_ref.shape[1:], jnp.float32)
            ref[0] = jnp.zeros(ref.shape[1:], jnp.float32)

    edge_ref[...] = jnp.zeros_like(edge_ref)

    column = lax.broadcasted_iota(jnp.int32, (BLOCK, LANES), 1)

    def prepare(f, odd):
        weight_ref = weight_refs[odd]
        live = (column // APER) == odd
        lanes = pl.ds(pl.multiple_of(f // 2 * LANES, LANES), LANES)
        for block in range(blocks):
            for x in range(2):
                cells = jnp.where(live, band_ref[x, block * BLOCK : (block + 1) * BLOCK, lanes], 0.0)
                cells = pltpu.roll(cells, shift_ref[block] + SHIFT + APER * odd, 1)
                for h in range(2):
                    taps = pltpu.roll(cells[h * HALF : (h + 1) * HALF], 0, 1, stride=1, stride_axis=0)
                    weight_ref[2 * block + h, 0, x], weight_ref[2 * block + h, 1, x] = split(taps)

    small[3].wait()
    prepare(0, 0)
    prepare(1, 1)

    pl.semaphore_wait(barrier, greeted)

    for f in range(FIRST):
        send_halos(f)

    @pl.when(has_below)
    def _():
        mask_copy(0).start()

    @pl.when(has_above)
    def _():
        mask_copy(1).start()

    lane = lax.broadcasted_iota(jnp.int32, (BLOCK, LANES), 1)

    def packed(block):
        return pl.ds(block // quarters * BLOCK, BLOCK), block % quarters * share

    for g in range(GROUPS):
        @pl.loop(0, group)
        def _(i):
            f = g * group + i
            load(f).wait()
            for chunk in range(0, blocks, quarters):
                rows, _ = packed(chunk)
                first, last = edge_ref[g, 0, rows, :], edge_ref[g, 1, rows, :]
                for block in range(chunk, min(chunk + quarters, blocks)):
                    cells = pl.ds(block * BLOCK, BLOCK)
                    for x in range(2):
                        place = packed(block)[1] + 4 * i + 2 * x
                        ours = (lane >= place) & (lane < place + 2)
                        first = jnp.where(ours, pltpu.roll(wave_ref[x, f, cells, :LANES], place, 1), first)
                        turned = pltpu.roll(wave_ref[x, f, cells, shots - LANES :], lax.rem(place + 2, LANES), 1)
                        last = jnp.where(ours, turned, last)
                edge_ref[g, 0, rows, :] = first
                edge_ref[g, 1, rows, :] = last

        @pl.when(has_next)
        def _():
            edge_copy(g, 0).start()

        @pl.when(has_prev)
        def _():
            edge_copy(g, 1).start()

    wide = lax.broadcasted_iota(jnp.int32, (HALO, LANES), 1)
    for end, block, skip in ((0, blocks - 1, BLOCK - HALO), (1, 0, 0)):
        cells = jnp.zeros((HALO, LANES), jnp.float32)
        rows, place = packed(block)
        for side in range(2):
            for g in range(GROUPS):
                spot = side * LANES // 2 + g * share
                part = pltpu.roll(edge_ref[g, side, rows, :][skip : skip + HALO], (spot - place) % LANES, 1)
                cells = jnp.where((wide >= spot) & (wide < spot + share), part, cells)
        ends_ref[end] = cells

    for i, there, came, peer, end in corners:
        @pl.when(there)
        def _():
            corner_copy(i, peer, end).start()

    @pl.loop(FIRST, slices)
    def _(f):
        send_halos(f)

    def turned(after, before, at_after, at_before):
        count = after.shape[0]
        after = pltpu.roll(after, lax.rem(LANES - at_after, LANES), 1)
        before = pltpu.roll(before, lax.rem(2 * LANES - 2 - at_before, LANES), 1)
        return jnp.where(lax.broadcasted_iota(jnp.int32, (count, LANES), 1) < LANES // 2, after, before)

    def stage(odd, x, wave, mask, outside, at):
        high_ref, low_ref = rows_refs[odd]
        count = wave.shape[0]
        tile = lax.broadcasted_iota(jnp.int32, (count, LANES), 1) < LANES // 2
        outside = split(outside * mask)
        inside = [split(wave[:, i * LANES : (i + 1) * LANES] * mask) for i in range(shots // LANES)]
        cells = [outside, *inside, outside]
        parts = []
        for part in range(2):
            rows = []
            for i in range(shots // LANES):
                around = jnp.where(tile, cells[i + 2][part], cells[i][part])
                rows.append(jnp.concatenate([cells[i + 1][part], around], axis=1))
            parts.append(jnp.concatenate(rows, axis=0))
        both = jnp.dot(jnp.concatenate(parts, axis=1), turn_ref[...], preferred_element_type=jnp.float32)
        high, low = split(both[:, :LANES] + both[:, LANES:])
        rows = pl.ds(at, count)
        for i in range(shots // LANES):
            lanes = pl.ds(i * LANES, LANES)
            high_ref[x, rows, lanes] = high[i * count : (i + 1) * count]
            low_ref[x, rows, lanes] = low[i * count : (i + 1) * count]

    def predict(f, odd, block):
        (high_ref, low_ref), weight_ref = rows_refs[odd], weight_refs[odd]
        total = jnp.zeros((8, shots), jnp.float32)
        for h in range(2):
            half = 2 * block + h
            base = half * HALF
            parts = []
            for part in range(2):
                real, imag = weight_ref[half, part, 0], weight_ref[half, part, 1]
                parts.append(jnp.concatenate([real, -imag], axis=1))
                parts.append(jnp.concatenate([imag, real], axis=1))
            window = pl.ds(base, DEPTH)
            high = jnp.concatenate([high_ref[x, window, :] for x in range(2)], axis=0)
            low = jnp.concatenate([low_ref[x, window, :] for x in range(2)], axis=0)
            upper = jnp.dot(jnp.concatenate(parts, axis=0), high, preferred_element_type=jnp.float32)
            lower = jnp.dot(jnp.concatenate(parts[:2], axis=0), low, preferred_element_type=jnp.float32)
            pred = upper[:BLOCK] + (upper[BLOCK:] + lower)
            for x in range(2):
                mult_ref[x, f, pl.ds(base, HALF), :] = pred[x * HALF : (x + 1) * HALF]
            total = total + jnp.sum((pred * pred).reshape(-1, 8, shots), axis=0)
        return total

    def lanes_of(total):
        return sum(total[:, i * LANES : (i + 1) * LANES] for i in range(shots // LANES))

    def wait_edges(g):
        @pl.when(has_prev)
        def _():
            edge_copy(g, 0).wait_recv()

        @pl.when(has_next)
        def _():
            edge_copy(g, 1).wait_recv()

    def wait_halos(f):
        @pl.when(has_above)
        def _():
            up(f).wait_recv()

        @pl.when(has_below)
        def _():
            down(f).wait_recv()

    def stage_own(f, odd):
        g, i = f // group, lax.rem(f, group)
        data = jnp.zeros((8, LANES), jnp.float32)
        for block in range(blocks):
            rows = pl.ds(block * BLOCK, BLOCK)
            cells, place = packed(block)
            after, before = next_ref[g, cells, :], prev_ref[g, cells, :]
            for x in range(2):
                wave = wave_ref[x, f, rows, :]
                at = place + 4 * i + 2 * x
                stage(odd, x, wave, mask_ref[rows, :], turned(after, before, at, at), block * BLOCK + HALO)
                data = data + lanes_of(jnp.sum((wave * wave).reshape(-1, 8, shots), axis=0))
        data_ref[f] = data

    def stage_halos(f, odd):
        for x in range(2):
            at = 4 * f + 2 * x
            for k, (ref, start, there) in enumerate(
                ((above_ref, 0, has_above), (below_ref, HALO + receivers, has_below))
            ):
                outside = turned(corner_ref[2 * k + 1], corner_ref[2 * k], at, LANES // 2 + at)
                stage(odd, x, ref[f * there.astype(jnp.int32), x], masks_ref[k], outside, start)

    def predict_inner(f, odd):
        total = jnp.zeros((8, shots), jnp.float32)
        for block in range(1, blocks - 1):
            total = total + predict(f, odd, block)
        inner_ref[f] = lanes_of(total)

    def predict_outer(f, odd):
        total = jnp.zeros((8, shots), jnp.float32)
        for block in sorted({0, blocks - 1}):
            total = total + predict(f, odd, block)
        outer_ref[f] = lanes_of(total)

    def step(f, odd):
        wait_halos(f)
        stage_halos(f, odd)
        stage_own(f + 1, 1 - odd)
        predict_outer(f, odd)
        predict_inner(f + 1, 1 - odd)

    wait_edges(0)
    stage_own(0, 0)
    predict_inner(0, 0)

    @pl.when(has_above)
    def _():
        mask_copy(0).wait_recv()

    @pl.when(has_below)
    def _():
        mask_copy(1).wait_recv()

    for i, there, came, peer, end in corners:
        @pl.when(came)
        def _():
            corner_copy(i, peer, end).wait_recv()

    @pl.loop(0, slices // 2 - 1)
    def _(pair):
        f = 2 * pair
        step(f, 0)
        prepare(f + 2, 0)
        for g in range(1, GROUPS):
            @pl.when(f + 2 == g * group)
            def _():
                wait_edges(g)

        step(f + 1, 1)
        prepare(f + 3, 1)

    step(slices - 2, 0)
    wait_halos(slices - 1)
    stage_halos(slices - 1, 1)
    predict_outer(slices - 1, 1)

    cells = jnp.concatenate([jnp.sum(data_ref[...], axis=1), jnp.sum(inner_ref[...] + outer_ref[...], axis=1)], axis=0)
    row = lax.broadcasted_iota(jnp.int32, cells.shape, 0)
    col = lax.broadcasted_iota(jnp.int32, cells.shape, 1)
    spot = jnp.where(row < slices, row, row - slices + LANES // 2)
    cells = jnp.where(col == spot, jnp.sum(cells, axis=1, keepdims=True), 0.0)
    mine = jnp.sum(cells, axis=0, keepdims=True)
    mine_ref[...] = mine

    def exchange(source, target, pairs, send, recv):
        copies = []
        for n, (a, b) in enumerate(pairs):
            copy = pltpu.make_async_remote_copy(
                src_ref=source, dst_ref=target.at[n], send_sem=send.at[n], recv_sem=recv.at[n],
                device_id=peer_of(a, b), device_id_type=MESH,
            )
            copy.start()
            copies.append(copy)
        for copy in copies:
            copy.wait()

    if direct:
        pairs = [(a, b) for b in range(fast_count) for a in range(slow_count) if a or b]
        exchange(mine_ref, space_ref, pairs, send_b, recv_b)
        total = mine + jnp.sum(space_ref[...], axis=0)
    else:
        exchange(mine_ref, plane_ref, [(a, 0) for a in range(1, slow_count)], send_a, recv_a)
        total = mine + jnp.sum(plane_ref[...], axis=0)
        mine_ref[...] = total
        exchange(mine_ref, space_ref, [(0, b) for b in range(1, fast_count)], send_b, recv_b)
        total = total + jnp.sum(space_ref[...], axis=0)
    gain_ref[...] = jnp.sqrt((total + 1e-06) / (pltpu.roll(total, LANES // 2, 1) + 1e-06))

    @pl.when(has_below)
    def _():
        mask_copy(0).wait_send()

        @pl.loop(0, slices)
        def _(f):
            up(f).wait_send()

    @pl.when(has_above)
    def _():
        mask_copy(1).wait_send()

        @pl.loop(0, slices)
        def _(f):
            down(f).wait_send()

    for g in range(GROUPS):
        @pl.when(has_next)
        def _():
            edge_copy(g, 0).wait_send()

        @pl.when(has_prev)
        def _():
            edge_copy(g, 1).wait_send()

    for i, there, came, peer, end in corners:
        @pl.when(there)
        def _():
            corner_copy(i, peer, end).wait_send()


def forward(axes, wave, band, shift, live, taper):
    _, slices, receivers, shots = wave.shape
    slow_count, fast_count = axes[0][1], axes[1][1]
    direct = slow_count * fast_count <= 32
    peers = slow_count * fast_count - 1 if direct else fast_count - 1
    tall = receivers + DEPTH - HALF
    blocks, quarters = receivers // BLOCK, LANES // (4 * slices // GROUPS)
    packed = -(-blocks // quarters) * BLOCK
    dma = pltpu.SemaphoreType.DMA
    whole = pl.BlockSpec(memory_space=pltpu.VMEM)
    hbm = pl.BlockSpec(memory_space=pltpu.HBM)
    return pl.pallas_call(
        functools.partial(forward_kernel, axes),
        in_specs=[hbm] * 5,
        out_specs=[whole, whole, whole],
        out_shape=[
            jax.ShapeDtypeStruct(wave.shape, jnp.float32),
            jax.ShapeDtypeStruct(wave.shape, jnp.float32),
            jax.ShapeDtypeStruct((1, LANES), jnp.float32),
        ],
        scratch_shapes=[
            pltpu.SMEM(shift.shape, jnp.int32),
            pltpu.SMEM(taper.shape, jnp.float32),
            pltpu.SMEM(live.shape, jnp.int32),
            pltpu.VMEM((receivers, LANES), jnp.float32),
            pltpu.VMEM(band.shape, jnp.float32),
            pltpu.VMEM((4 * LANES, 2 * LANES), jnp.bfloat16),
            *[pltpu.VMEM((receivers // HALF, 2, 2, HALF, DEPTH), jnp.bfloat16)] * 2,
            *[pltpu.VMEM((2, tall, shots), jnp.bfloat16)] * 4,
            pltpu.VMEM((slices, 2, HALO, shots), jnp.float32),
            pltpu.VMEM((slices, 2, HALO, shots), jnp.float32),
            pltpu.VMEM((GROUPS, 2, packed, LANES), jnp.float32),
            pltpu.VMEM((GROUPS, packed, LANES), jnp.float32),
            pltpu.VMEM((GROUPS, packed, LANES), jnp.float32),
            pltpu.VMEM((2, HALO, LANES), jnp.float32),
            pltpu.VMEM((4, HALO, LANES), jnp.float32),
            pltpu.VMEM((2, HALO, LANES), jnp.float32),
            *[pltpu.VMEM((slices, 8, LANES), jnp.float32)] * 3,
            pltpu.VMEM((1, LANES), jnp.float32),
            pltpu.VMEM((slow_count - 1, 1, LANES), jnp.float32),
            pltpu.VMEM((peers, 1, LANES), jnp.float32),
            dma((slices,)), dma((4,)), dma((slices,)), dma((slices,)), dma((slices,)), dma((slices,)),
            dma((2,)), dma((2,)), dma((GROUPS, 2)), dma((GROUPS, 2)), dma((4,)), dma((4,)),
            dma((slow_count - 1,)), dma((slow_count - 1,)), dma((peers,)), dma((peers,)),
        ],
        cost_estimate=pl.CostEstimate(flops=2**33, bytes_accessed=wave.size * 8, transcendentals=0),
        compiler_params=pltpu.CompilerParams(
            collective_id=1, has_side_effects=True, vmem_limit_bytes=14 * 2**20
        ),
        name="forward",
    )(shift, taper, live, wave, band)


def finish_kernel(gain_ref, wave_ref, mult_ref, mult_hbm, prim_hbm, prim_ref, mult_sem, prim_sem):
    slices = wave_ref.shape[1]
    slots = prim_ref.shape[0]

    def mult_copy(f):
        return pltpu.make_async_copy(mult_ref.at[:, f], mult_hbm.at[:, f], mult_sem.at[f])

    def prim_copy(f):
        return pltpu.make_async_copy(prim_ref.at[lax.rem(f, slots)], prim_hbm.at[:, f], prim_sem.at[f])

    col = lax.broadcasted_iota(jnp.int32, (1, LANES), 1)

    @pl.loop(0, slices)
    def _(f):
        mult_copy(f).start()
        gain = jnp.sum(jnp.where(col == f, gain_ref[...], 0.0))

        @pl.when(f >= slots)
        def _():
            prim_copy(f - slots).wait()

        for x in range(2):
            for r in range(0, wave_ref.shape[2], BLOCK):
                rows = pl.ds(r, BLOCK)
                prim_ref[lax.rem(f, slots), x, rows, :] = wave_ref[x, f, rows, :] - gain * mult_ref[x, f, rows, :]
        prim_copy(f).start()

    @pl.loop(0, slices)
    def _(f):
        mult_copy(f).wait()

    @pl.loop(max(slices - slots, 0), slices)
    def _(f):
        prim_copy(f).wait()


def finish(gain, wave, mult):
    slices = wave.shape[1]
    whole = pl.BlockSpec(memory_space=pltpu.VMEM)
    hbm = pl.BlockSpec(memory_space=pl.ANY)
    return pl.pallas_call(
        finish_kernel,
        in_specs=[whole, whole, whole],
        out_specs=[hbm, hbm],
        out_shape=[jax.ShapeDtypeStruct(wave.shape, jnp.float32)] * 2,
        scratch_shapes=[
            pltpu.VMEM((min(SLOTS, slices), 2, *wave.shape[2:]), jnp.float32),
            pltpu.SemaphoreType.DMA((slices,)),
            pltpu.SemaphoreType.DMA((slices,)),
        ],
        cost_estimate=pl.CostEstimate(flops=wave.size * 2, bytes_accessed=wave.size * 8, transcendentals=0),
        compiler_params=pltpu.CompilerParams(vmem_limit_bytes=12 * 2**20),
        name="finish",
    )(gain, wave, mult)


def per_device(wavefield, surface_band, band_shift, trace_mask, shot_taper):
    axes = (("src", lax.axis_size("src")), ("rcv", lax.axis_size("rcv")))
    def keep(array):
        return pltpu.with_memory_space_constraint(array, pltpu.HBM) if array.size > 1 else array

    small = [keep(array) for array in (surface_band, band_shift, trace_mask, shot_taper)]
    wave, mult, gain = forward(axes, wavefield, *small)
    return tuple(finish(gain, wave, mult))


def solution(mesh):
    in_specs = (P(None, None, "rcv", "src"), P(None, "rcv", None), P("rcv"), P("rcv"), P())
    out_specs = (P(None, None, "rcv", "src"), P(None, None, "rcv", "src"))
    return jax.shard_map(
        per_device, mesh=mesh, in_specs=in_specs, out_specs=out_specs, check_vma=False
    )
```

time: 78.8 us -> 62 us (0.79)
  Pallas kernels: 74.3 us -> 61.2 us
  local copies, waits for them, and re-layouts: 2.99 us -> 0 us
    pallas_call x1, Pallas kernels: 63.1 us -> 50.1 us  [forward(): pl.pallas_call(functools.partial(forward_kernel, axes), in_specs=[hbm] *...]
    unnamed x6 -> x0, local copies, waits for them, and re-layouts: 2.9 us -> none
where the time goes in v2:
time: 62 us; the launch traced here: 61.9 us
  Pallas kernels  61.2 us (99%)
  between operations  0.64 us (1%)
    pallas_call x1, Pallas kernels, forward(): pl.pallas_call(functools.partial(forward_kernel, axes), in_specs=[hbm] *...  50.1 us
    pallas_call x1, Pallas kernels, finish(): pl.pallas_call(finish_kernel, in_specs=[whole, whole, whole], out_specs=[...  11.2 us

profile of v2, /device:TPU:0, one launch (start us, length us, event | category | flops | bytes accessed | tf_op | source)
XLA Modules:
  0.0 61.9 jit_solution(5134712206041567613)
XLA Ops:
  0.6 50.1 %forward.1 = (f32[2,16,256,512]{3,2,1,0:T(8,128)S(1)}, f32[2,16,256,512]{3,2,1,0:T(8,128)S(1)}, f32[1,128]{1,0:T(1,128)S(1)}) custom-call(s32[4]{0:T(128)} %shift_hbm.1, f32[5]{0:T(128)} %taper_hbm.1, s32[256]{0:T(256)} %live_hbm.1, f32[2,16,256,512]{3,2,1,0:T(8,128)} %wave_hbm.1, f32[2,256,1024]{2,1,0:T(8,128)} %band_hbm.1), custom_call_target="tpu_custom_call" | custom-call | flops 8589934592 | bytes 33554432 | tf_op jit(solution)/shard_map/forward/pallas_call | solution.py:493
  50.7 11.2 %finish.1 = (f32[2,16,256,512]{3,2,1,0:T(8,128)}, f32[2,16,256,512]{3,2,1,0:T(8,128)}) custom-call(f32[1,128]{1,0:T(1,128)S(1)} %get-tuple-element.5.gain_ref, f32[2,16,256,512]{3,2,1,0:T(8,128)S(1)} %get-tuple-element.6.wave_ref, f32[2,16,256,512]{3,2,1,0:T(8,128)S(1)} %get-tuple-element.7.mult_ref), custom_call_target="tpu_custom_call" | custom-call | flops 8388608 | bytes 33554432 | tf_op jit(solution)/shard_map/finish/pallas_call | solution.py:575

commit v3 on v2

--- a/solution.py
+++ b/solution.py
@@ -35,7 +35,7 @@
         even_weight, odd_weight, even_high, odd_high, even_low, odd_low, above_ref, below_ref, edge_ref, next_ref, prev_ref, ends_ref, corner_ref, masks_ref,
         data_ref, inner_ref, outer_ref, mine_ref, plane_ref, space_ref,
         load_sem, small_sem, send_up, recv_up, send_down, recv_down, send_mask, recv_mask,
-        send_edge, recv_edge, send_corner, recv_corner, send_a, recv_a, send_b, recv_b,
+        send_edge, recv_edge, send_corner, recv_corner, send_a, recv_a, send_b, recv_b, flood_sem,
     ) = refs[3:]
     (slow, slow_count), (fast, fast_count) = axes
     slow_me, fast_me = lax.axis_index(slow), lax.axis_index(fast)
@@ -112,22 +112,16 @@
     for copy in small[:3]:
         copy.start()
     barrier = pltpu.get_barrier_semaphore()
-    if direct:
-        greeted = slow_count * fast_count - 1
-        for a in range(slow_count):
-            for b in range(fast_count):
-                if a or b:
-                    pl.semaphore_signal(barrier, inc=1, device_id=peer_of(a, b), device_id_type=MESH)
-    else:
-        greeted = slow_count + fast_count - 2 + sum(there.astype(jnp.int32) for _, there, *_ in corners)
-        for a in range(1, slow_count):
-            pl.semaphore_signal(barrier, inc=1, device_id=peer_of(a, 0), device_id_type=MESH)
-        for b in range(1, fast_count):
-            pl.semaphore_signal(barrier, inc=1, device_id=peer_of(0, b), device_id_type=MESH)
-        for i, there, came, peer, end in corners:
-            @pl.when(there)
-            def _():
-                pl.semaphore_signal(barrier, inc=1, device_id=peer, device_id_type=MESH)
+    near = [
+        (has_above, {fast: fast_me - 1}), (has_below, {fast: fast_me + 1}),
+        (has_prev, {slow: slow_me - 1}), (has_next, {slow: slow_me + 1}),
+    ]
+    beside = sum(there.astype(jnp.int32) for there, _ in near)
+    greeted = beside + sum(there.astype(jnp.int32) for _, there, *_ in corners)
+    for there, peer in near + [(there, peer) for _, there, _, peer, _ in corners]:
+        @pl.when(there)
+        def _():
+            pl.semaphore_signal(barrier, inc=1, device_id=peer, device_id_type=MESH)
 
     small[3].start()
 
@@ -135,15 +129,28 @@
     def _(f):
         load(f).start()
 
+    pl.semaphore_wait(barrier, greeted)
+
+    for f in range(FIRST):
+        send_halos(f)
+
     small[0].wait()
     line = lax.broadcasted_iota(jnp.int32, (8, LANES), 0)
 
-    @pl.loop(0, receivers // 8)
+    @pl.loop(0, receivers // 8, unroll=4)
     def _(i):
         cells = jnp.zeros((8, LANES), jnp.float32)
         for r in range(8):
             cells = jnp.where(line == r, live_ref[i * 8 + r].astype(jnp.float32), cells)
         mask_ref[pl.ds(pl.multiple_of(i * 8, 8), 8), :] = cells
+
+    @pl.when(has_below)
+    def _():
+        mask_copy(0).start()
+
+    @pl.when(has_above)
+    def _():
+        mask_copy(1).start()
 
     small[1].wait()
     small[2].wait()
@@ -159,14 +166,6 @@
         turn_ref[2 * i * LANES : 2 * (i + 1) * LANES, :] = turn
 
     rows_refs, weight_refs = ((even_high, even_low), (odd_high, odd_low)), (even_weight, odd_weight)
-    zeros = jnp.zeros((STRIP, shots), jnp.bfloat16)
-    for x in range(2):
-        @pl.loop(0, even_high.shape[1] // STRIP)
-        def _(i):
-            rows = pl.ds(pl.multiple_of(i * STRIP, STRIP), STRIP)
-            for ref in (even_high, odd_high, even_low, odd_low):
-                ref[x, rows, :] = zeros
-
     for there, ref in ((has_prev, prev_ref), (has_next, next_ref)):
         @pl.when(jnp.logical_not(there))
         def _():
@@ -201,20 +200,6 @@
 
     small[3].wait()
     prepare(0, 0)
-    prepare(1, 1)
-
-    pl.semaphore_wait(barrier, greeted)
-
-    for f in range(FIRST):
-        send_halos(f)
-
-    @pl.when(has_below)
-    def _():
-        mask_copy(0).start()
-
-    @pl.when(has_above)
-    def _():
-        mask_copy(1).start()
 
     lane = lax.broadcasted_iota(jnp.int32, (BLOCK, LANES), 1)
 
@@ -222,7 +207,7 @@
         return pl.ds(block // quarters * BLOCK, BLOCK), block % quarters * share
 
     for g in range(GROUPS):
-        @pl.loop(0, group)
+        @pl.loop(0, group, unroll=2)
         def _(i):
             f = g * group + i
             load(f).wait()
@@ -374,7 +359,18 @@
             total = total + predict(f, odd, block)
         outer_ref[f] = lanes_of(total)
 
+    def flood(n):
+        for there, peer in near:
+            @pl.when(there)
+            def _():
+                pl.semaphore_signal(flood_sem.at[n], inc=1, device_id=peer, device_id_type=MESH)
+
     def step(f, odd):
+        @pl.when(f > 0)
+        def _():
+            pl.semaphore_wait(flood_sem.at[f - 1], beside)
+
+        flood(f)
         wait_halos(f)
         stage_halos(f, odd)
         stage_own(f + 1, 1 - odd)
@@ -383,6 +379,7 @@
 
     wait_edges(0)
     stage_own(0, 0)
+    prepare(1, 1)
     predict_inner(0, 0)
 
     @pl.when(has_above)
@@ -412,9 +409,13 @@
         prepare(f + 3, 1)
 
     step(slices - 2, 0)
+    pl.semaphore_wait(flood_sem.at[slices - 2], beside)
     wait_halos(slices - 1)
     stage_halos(slices - 1, 1)
     predict_outer(slices - 1, 1)
+    for n in range(slices - 1, flood_sem.shape[0]):
+        flood(n)
+        pl.semaphore_wait(flood_sem.at[n], beside)
 
     cells = jnp.concatenate([jnp.sum(data_ref[...], axis=1), jnp.sum(inner_ref[...] + outer_ref[...], axis=1)], axis=0)
     row = lax.broadcasted_iota(jnp.int32, cells.shape, 0)
@@ -484,6 +485,7 @@
     slow_count, fast_count = axes[0][1], axes[1][1]
     direct = slow_count * fast_count <= 32
     peers = slow_count * fast_count - 1 if direct else fast_count - 1
+    farthest = slow_count + fast_count - 2 if direct else max(slow_count, fast_count) - 1
     tall = receivers + DEPTH - HALF
     blocks, quarters = receivers // BLOCK, LANES // (4 * slices // GROUPS)
     packed = -(-blocks // quarters) * BLOCK
@@ -523,6 +525,7 @@
             dma((slices,)), dma((4,)), dma((slices,)), dma((slices,)), dma((slices,)), dma((slices,)),
             dma((2,)), dma((2,)), dma((GROUPS, 2)), dma((GROUPS, 2)), dma((4,)), dma((4,)),
             dma((slow_count - 1,)), dma((slow_count - 1,)), dma((peers,)), dma((peers,)),
+            pltpu.SemaphoreType.REGULAR((max(slices, farthest) - 1,)),
         ],
         cost_estimate=pl.CostEstimate(flops=2**33, bytes_accessed=wave.size * 8, transcendentals=0),
         compiler_params=pltpu.CompilerParams(

time: 62 us -> 61.1 us (0.985)
  Pallas kernels: 61.2 us -> 60.3 us
    pallas_call x1, Pallas kernels: 50.1 us -> 49.2 us  [forward(): pl.pallas_call(functools.partial(forward_kernel, axes), in_specs=[hbm] *...]
where the time goes in v3:
time: 61.1 us; the launch traced here: 60.9 us
  Pallas kernels  60.3 us (99%)
  between operations  0.64 us (1%)
    pallas_call x1, Pallas kernels, forward(): pl.pallas_call(functools.partial(forward_kernel, axes), in_specs=[hbm] *...  49.2 us
    pallas_call x1, Pallas kernels, finish(): pl.pallas_call(finish_kernel, in_specs=[whole, whole, whole], out_specs=[...  11.2 us

profile of v3, /device:TPU:0, one launch (start us, length us, event | category | flops | bytes accessed | tf_op | source)
XLA Modules:
  0.0 60.9 jit_solution(3929391228495816197)
XLA Ops:
  0.6 49.2 %forward.1 = (f32[2,16,256,512]{3,2,1,0:T(8,128)S(1)}, f32[2,16,256,512]{3,2,1,0:T(8,128)S(1)}, f32[1,128]{1,0:T(1,128)S(1)}) custom-call(s32[4]{0:T(128)} %shift_hbm.1, f32[5]{0:T(128)} %taper_hbm.1, s32[256]{0:T(256)} %live_hbm.1, f32[2,16,256,512]{3,2,1,0:T(8,128)} %wave_hbm.1, f32[2,256,1024]{2,1,0:T(8,128)} %band_hbm.1), custom_call_target="tpu_custom_call" | custom-call | flops 8589934592 | bytes 33554432 | tf_op jit(solution)/shard_map/forward/pallas_call | solution.py:495
  49.8 11.2 %finish.1 = (f32[2,16,256,512]{3,2,1,0:T(8,128)}, f32[2,16,256,512]{3,2,1,0:T(8,128)}) custom-call(f32[1,128]{1,0:T(1,128)S(1)} %get-tuple-element.5.gain_ref, f32[2,16,256,512]{3,2,1,0:T(8,128)S(1)} %get-tuple-element.6.wave_ref, f32[2,16,256,512]{3,2,1,0:T(8,128)S(1)} %get-tuple-element.7.mult_ref), custom_call_target="tpu_custom_call" | custom-call | flops 8388608 | bytes 33554432 | tf_op jit(solution)/shard_map/finish/pallas_call | solution.py:578

commit v4 on v3

--- a/solution.py
+++ b/solution.py
@@ -15,7 +15,7 @@
 LANES = 128
 DEPTH = 128
 HALO = APER // 2 + SHIFT
-FIRST = 3
+FIRST = 2
 GROUPS = 2
 STRIP = 16
 SLOTS = 8
@@ -32,7 +32,7 @@
     wave_ref, mult_ref, gain_ref = refs[:3]
     (
         shift_ref, taper_ref, live_ref, mask_ref, band_ref, turn_ref,
-        even_weight, odd_weight, even_high, odd_high, even_low, odd_low, above_ref, below_ref, edge_ref, next_ref, prev_ref, ends_ref, corner_ref, masks_ref,
+        even_weight, odd_weight, even_high, odd_high, even_low, odd_low, above_ref, below_ref, edge_ref, next_ref, prev_ref, ends_ref, corner_ref, masks_ref, line_ref, came_ref,
         data_ref, inner_ref, outer_ref, mine_ref, plane_ref, space_ref,
         load_sem, small_sem, send_up, recv_up, send_down, recv_down, send_mask, recv_mask,
         send_edge, recv_edge, send_corner, recv_corner, send_a, recv_a, send_b, recv_b, flood_sem,
@@ -56,8 +56,16 @@
         came = (has_above if down > 0 else has_below) & (has_prev if right > 0 else has_next)
         corners.append((i, there, came, {fast: fast_me + down, slow: slow_me + right}, 0 if down > 0 else 1))
 
-    def load(f):
-        return pltpu.make_async_copy(wave_hbm.at[:, f], wave_ref.at[:, f], load_sem.at[f])
+    spans = [(0, LANES), (shots - LANES, LANES), (LANES, shots - 2 * LANES)]
+    spans = [pl.ds(start, count) for start, count in spans if count > 0]
+
+    def load(f, part):
+        cells = (slice(None), f, slice(None), spans[part])
+        return pltpu.make_async_copy(wave_hbm.at[cells], wave_ref.at[cells], load_sem.at[part, f])
+
+    def wait_rest(f):
+        for part in range(2, len(spans)):
+            load(f, part).wait()
 
     def up(f):
         return pltpu.make_async_remote_copy(
@@ -75,7 +83,7 @@
 
     def mask_copy(i):
         return pltpu.make_async_remote_copy(
-            src_ref=mask_ref.at[pl.ds(0 if i else receivers - HALO, HALO)], dst_ref=masks_ref.at[i],
+            src_ref=line_ref.at[i], dst_ref=came_ref.at[i],
             send_sem=send_mask.at[i], recv_sem=recv_mask.at[i],
             device_id={fast: fast_me - 1 if i else fast_me + 1}, device_id_type=MESH,
         )
@@ -89,7 +97,7 @@
 
     def corner_copy(i, peer, end):
         return pltpu.make_async_remote_copy(
-            src_ref=ends_ref.at[end], dst_ref=corner_ref.at[i],
+            src_ref=ends_ref.at[end, 1 - i % 2], dst_ref=corner_ref.at[i],
             send_sem=send_corner.at[i], recv_sem=recv_corner.at[i],
             device_id=peer, device_id_type=MESH,
         )
@@ -125,9 +133,11 @@
 
     small[3].start()
 
-    @pl.loop(0, slices)
-    def _(f):
-        load(f).start()
+    for parts in (range(2), range(2, len(spans))):
+        @pl.loop(0, slices)
+        def _(f):
+            for part in parts:
+                load(f, part).start()
 
     pl.semaphore_wait(barrier, greeted)
 
@@ -143,6 +153,11 @@
         for r in range(8):
             cells = jnp.where(line == r, live_ref[i * 8 + r].astype(jnp.float32), cells)
         mask_ref[pl.ds(pl.multiple_of(i * 8, 8), 8), :] = cells
+
+    diagonal = lax.broadcasted_iota(jnp.int32, (HALO, LANES), 0) == lax.broadcasted_iota(jnp.int32, (HALO, LANES), 1)
+    for i, start in enumerate((receivers - HALO, 0)):
+        cells = jnp.where(diagonal, mask_ref[start : start + HALO, :], 0.0)
+        line_ref[i] = jnp.sum(cells, axis=0, keepdims=True)
 
     @pl.when(has_below)
     def _():
@@ -179,7 +194,7 @@
     for i, (there, ref) in enumerate(((has_above, above_ref), (has_below, below_ref))):
         @pl.when(jnp.logical_not(there))
         def _():
-            masks_ref[i] = jnp.zeros(masks_ref.shape[1:], jnp.float32)
+            came_ref[i] = jnp.zeros(came_ref.shape[1:], jnp.float32)
             ref[0] = jnp.zeros(ref.shape[1:], jnp.float32)
 
     edge_ref[...] = jnp.zeros_like(edge_ref)
@@ -210,7 +225,8 @@
         @pl.loop(0, group, unroll=2)
         def _(i):
             f = g * group + i
-            load(f).wait()
+            load(f, 0).wait()
+            load(f, 1).wait()
             for chunk in range(0, blocks, quarters):
                 rows, _ = packed(chunk)
                 first, last = edge_ref[g, 0, rows, :], edge_ref[g, 1, rows, :]
@@ -233,16 +249,18 @@
         def _():
             edge_copy(g, 1).start()
 
+    fold = HALO // 2
     wide = lax.broadcasted_iota(jnp.int32, (HALO, LANES), 1)
     for end, block, skip in ((0, blocks - 1, BLOCK - HALO), (1, 0, 0)):
-        cells = jnp.zeros((HALO, LANES), jnp.float32)
         rows, place = packed(block)
         for side in range(2):
+            cells = jnp.zeros((HALO, LANES), jnp.float32)
             for g in range(GROUPS):
-                spot = side * LANES // 2 + g * share
-                part = pltpu.roll(edge_ref[g, side, rows, :][skip : skip + HALO], (spot - place) % LANES, 1)
-                cells = jnp.where((wide >= spot) & (wide < spot + share), part, cells)
-        ends_ref[end] = cells
+                part = pltpu.roll(edge_ref[g, side, rows, :][skip : skip + HALO], (g * share - place) % LANES, 1)
+                cells = jnp.where((wide >= g * share) & (wide < (g + 1) * share), part, cells)
+            ends_ref[end, side] = jnp.where(
+                wide[:fold] < LANES // 2, cells[:fold], pltpu.roll(cells[fold:], LANES // 2, 1)
+            )
 
     for i, there, came, peer, end in corners:
         @pl.when(there)
@@ -315,14 +333,11 @@
         def _():
             edge_copy(g, 1).wait_recv()
 
-    def wait_halos(f):
-        @pl.when(has_above)
-        def _():
-            up(f).wait_recv()
-
-        @pl.when(has_below)
-        def _():
-            down(f).wait_recv()
+    def wait_halos(f, sides=(0, 1)):
+        for side in sides:
+            @pl.when(has_below if side else has_above)
+            def _():
+                (down if side else up)(f).wait_recv()
 
     def stage_own(f, odd):
         g, i = f // group, lax.rem(f, group)
@@ -338,13 +353,13 @@
                 data = data + lanes_of(jnp.sum((wave * wave).reshape(-1, 8, shots), axis=0))
         data_ref[f] = data
 
-    def stage_halos(f, odd):
+    def stage_halos(f, odd, sides=(0, 1)):
         for x in range(2):
             at = 4 * f + 2 * x
-            for k, (ref, start, there) in enumerate(
-                ((above_ref, 0, has_above), (below_ref, HALO + receivers, has_below))
-            ):
-                outside = turned(corner_ref[2 * k + 1], corner_ref[2 * k], at, LANES // 2 + at)
+            for k in sides:
+                ref, start, there = ((above_ref, 0, has_above), (below_ref, HALO + receivers, has_below))[k]
+                ends = [turned(corner_ref[2 * k + 1], corner_ref[2 * k], at + c, at + c) for c in (0, LANES // 2)]
+                outside = jnp.concatenate(ends, axis=0)
                 stage(odd, x, ref[f * there.astype(jnp.int32), x], masks_ref[k], outside, start)
 
     def predict_inner(f, odd):
@@ -371,6 +386,7 @@
             pl.semaphore_wait(flood_sem.at[f - 1], beside)
 
         flood(f)
+        wait_rest(f + 1)
         wait_halos(f)
         stage_halos(f, odd)
         stage_own(f + 1, 1 - odd)
@@ -378,6 +394,7 @@
         predict_inner(f + 1, 1 - odd)
 
     wait_edges(0)
+    wait_rest(0)
     stage_own(0, 0)
     prepare(1, 1)
     predict_inner(0, 0)
@@ -394,6 +411,10 @@
         @pl.when(came)
         def _():
             corner_copy(i, peer, end).wait_recv()
+
+    for i in range(2):
+        cells = jnp.sum(jnp.where(diagonal, came_ref[i], 0.0), axis=1, keepdims=True)
+        masks_ref[i] = jnp.broadcast_to(cells, masks_ref.shape[1:])
 
     @pl.loop(0, slices // 2 - 1)
     def _(pair):
@@ -410,19 +431,35 @@
 
     step(slices - 2, 0)
     pl.semaphore_wait(flood_sem.at[slices - 2], beside)
-    wait_halos(slices - 1)
-    stage_halos(slices - 1, 1)
-    predict_outer(slices - 1, 1)
-    for n in range(slices - 1, flood_sem.shape[0]):
-        flood(n)
-        pl.semaphore_wait(flood_sem.at[n], beside)
-
+
+    last = slices - 1
+    outer_ref[last] = jnp.zeros((8, LANES), jnp.float32)
     cells = jnp.concatenate([jnp.sum(data_ref[...], axis=1), jnp.sum(inner_ref[...] + outer_ref[...], axis=1)], axis=0)
     row = lax.broadcasted_iota(jnp.int32, cells.shape, 0)
     col = lax.broadcasted_iota(jnp.int32, cells.shape, 1)
     spot = jnp.where(row < slices, row, row - slices + LANES // 2)
     cells = jnp.where(col == spot, jnp.sum(cells, axis=1, keepdims=True), 0.0)
-    mine = jnp.sum(cells, axis=0, keepdims=True)
+    mine_ref[...] = jnp.sum(cells, axis=0, keepdims=True)
+
+    if blocks > 1:
+        for parity, sides in ((0, (1, 0)), (1, (0, 1))):
+            @pl.when(lax.rem(fast_me, 2) == parity)
+            def _():
+                for side in sides:
+                    wait_halos(last, (side,))
+                    stage_halos(last, 1, (side,))
+                    outer_ref[last] += lanes_of(predict(last, 1, (blocks - 1) * side))
+    else:
+        wait_halos(last)
+        stage_halos(last, 1)
+        predict_outer(last, 1)
+    for n in range(slices - 1, flood_sem.shape[0]):
+        flood(n)
+        pl.semaphore_wait(flood_sem.at[n], beside)
+
+    tail = jnp.sum(jnp.sum(outer_ref[last], axis=0, keepdims=True), axis=1, keepdims=True)
+    spot = lax.broadcasted_iota(jnp.int32, (1, LANES), 1) == LANES // 2 + last
+    mine = mine_ref[...] + jnp.where(spot, tail, 0.0)
     mine_ref[...] = mine
 
     def exchange(source, target, pairs, send, recv):
@@ -515,14 +552,16 @@
             pltpu.VMEM((GROUPS, 2, packed, LANES), jnp.float32),
             pltpu.VMEM((GROUPS, packed, LANES), jnp.float32),
             pltpu.VMEM((GROUPS, packed, LANES), jnp.float32),
+            pltpu.VMEM((2, 2, HALO // 2, LANES), jnp.float32),
+            pltpu.VMEM((4, HALO // 2, LANES), jnp.float32),
             pltpu.VMEM((2, HALO, LANES), jnp.float32),
-            pltpu.VMEM((4, HALO, LANES), jnp.float32),
-            pltpu.VMEM((2, HALO, LANES), jnp.float32),
+            pltpu.VMEM((2, 1, LANES), jnp.float32),
+            pltpu.VMEM((2, 1, LANES), jnp.float32),
             *[pltpu.VMEM((slices, 8, LANES), jnp.float32)] * 3,
             pltpu.VMEM((1, LANES), jnp.float32),
             pltpu.VMEM((slow_count - 1, 1, LANES), jnp.float32),
             pltpu.VMEM((peers, 1, LANES), jnp.float32),
-            dma((slices,)), dma((4,)), dma((slices,)), dma((slices,)), dma((slices,)), dma((slices,)),
+            dma((3, slices)), dma((4,)), dma((slices,)), dma((slices,)), dma((slices,)), dma((slices,)),
             dma((2,)), dma((2,)), dma((GROUPS, 2)), dma((GROUPS, 2)), dma((4,)), dma((4,)),
             dma((slow_count - 1,)), dma((slow_count - 1,)), dma((peers,)), dma((peers,)),
             pltpu.SemaphoreType.REGULAR((max(slices, farthest) - 1,)),

time: 61.1 us -> 60.9 us (level)
  no operation moved by 1% of the time
where the time goes in v4:
time: 60.9 us; the launch traced here: 60.8 us
  Pallas kernels  60.1 us (99%)
  between operations  0.64 us (1%)
    pallas_call x1, Pallas kernels, forward(): pl.pallas_call(functools.partial(forward_kernel, axes), in_specs=[hbm] *...  49 us
    pallas_call x1, Pallas kernels, finish(): pl.pallas_call(finish_kernel, in_specs=[whole, whole, whole], out_specs=[...  11.2 us

profile of v4, /device:TPU:0, one launch (start us, length us, event | category | flops | bytes accessed | tf_op | source)
XLA Modules:
  0.0 60.8 jit_solution(18314534480055132595)
XLA Ops:
  0.6 49.0 %forward.1 = (f32[2,16,256,512]{3,2,1,0:T(8,128)S(1)}, f32[2,16,256,512]{3,2,1,0:T(8,128)S(1)}, f32[1,128]{1,0:T(1,128)S(1)}) custom-call(s32[4]{0:T(128)} %shift_hbm.1, f32[5]{0:T(128)} %taper_hbm.1, s32[256]{0:T(256)} %live_hbm.1, f32[2,16,256,512]{3,2,1,0:T(8,128)} %wave_hbm.1, f32[2,256,1024]{2,1,0:T(8,128)} %band_hbm.1), custom_call_target="tpu_custom_call" | custom-call | flops 8589934592 | bytes 33554432 | tf_op jit(solution)/shard_map/forward/pallas_call | solution.py:532
  49.6 11.2 %finish.1 = (f32[2,16,256,512]{3,2,1,0:T(8,128)}, f32[2,16,256,512]{3,2,1,0:T(8,128)}) custom-call(f32[1,128]{1,0:T(1,128)S(1)} %get-tuple-element.5.gain_ref, f32[2,16,256,512]{3,2,1,0:T(8,128)S(1)} %get-tuple-element.6.wave_ref, f32[2,16,256,512]{3,2,1,0:T(8,128)S(1)} %get-tuple-element.7.mult_ref), custom_call_target="tpu_custom_call" | custom-call | flops 8388608 | bytes 33554432 | tf_op jit(solution)/shard_map/finish/pallas_call | solution.py:617

commit v5 on v4

--- a/solution.py
+++ b/solution.py
@@ -476,6 +476,7 @@
 
     if direct:
         pairs = [(a, b) for b in range(fast_count) for a in range(slow_count) if a or b]
+        pairs.sort(key=lambda pair: min(pair[1], fast_count - pair[1]) or fast_count)
         exchange(mine_ref, space_ref, pairs, send_b, recv_b)
         total = mine + jnp.sum(space_ref[...], axis=0)
     else:

time: 60.9 us -> 60.9 us (level)
  no operation moved by 1% of the time
where the time goes in v5:
time: 60.9 us; the launch traced here: 60.8 us
  Pallas kernels  60.2 us (99%)
  between operations  0.64 us (1%)
    pallas_call x1, Pallas kernels, forward(): pl.pallas_call(functools.partial(forward_kernel, axes), in_specs=[hbm] *...  49 us
    pallas_call x1, Pallas kernels, finish(): pl.pallas_call(finish_kernel, in_specs=[whole, whole, whole], out_specs=[...  11.2 us

profile of v5, /device:TPU:0, one launch (start us, length us, event | category | flops | bytes accessed | tf_op | source)
XLA Modules:
  0.0 60.8 jit_solution(570066979919401806)
XLA Ops:
  0.6 49.0 %forward.1 = (f32[2,16,256,512]{3,2,1,0:T(8,128)S(1)}, f32[2,16,256,512]{3,2,1,0:T(8,128)S(1)}, f32[1,128]{1,0:T(1,128)S(1)}) custom-call(s32[4]{0:T(128)} %shift_hbm.1, f32[5]{0:T(128)} %taper_hbm.1, s32[256]{0:T(256)} %live_hbm.1, f32[2,16,256,512]{3,2,1,0:T(8,128)} %wave_hbm.1, f32[2,256,1024]{2,1,0:T(8,128)} %band_hbm.1), custom_call_target="tpu_custom_call" | custom-call | flops 8589934592 | bytes 33554432 | tf_op jit(solution)/shard_map/forward/pallas_call | solution.py:533
  49.6 11.2 %finish.1 = (f32[2,16,256,512]{3,2,1,0:T(8,128)}, f32[2,16,256,512]{3,2,1,0:T(8,128)}) custom-call(f32[1,128]{1,0:T(1,128)S(1)} %get-tuple-element.5.gain_ref, f32[2,16,256,512]{3,2,1,0:T(8,128)S(1)} %get-tuple-element.6.wave_ref, f32[2,16,256,512]{3,2,1,0:T(8,128)S(1)} %get-tuple-element.7.mult_ref), custom_call_target="tpu_custom_call" | custom-call | flops 8388608 | bytes 33554432 | tf_op jit(solution)/shard_map/finish/pallas_call | solution.py:618
